TPU v7x, 32 devices: a whole 2x2x4 slice. The times are simulated.
32 devices in a mesh: data: 8 (over z, y), stage: 4 (over x, core).
Axes of the slice: x: 2, y: 2, z: 4, core: 2. Of those that a mesh axis runs over, the one named last changes fastest.
Arguments:
- master_up: float32 [4, 768, 3072], P('stage')
- master_down: float32 [4, 3072, 768], P('stage')
- mom1_up: float32 [4, 768, 3072], P('stage')
- mom1_down: float32 [4, 3072, 768], P('stage')
- mom2_up: float32 [4, 768, 3072], P('stage')
- mom2_down: float32 [4, 3072, 768], P('stage')
- grad_up: float32 [8, 4, 768, 3072], P('data', 'stage')
- grad_down: float32 [8, 4, 3072, 768], P('data', 'stage')
- stage_acts: bfloat16 [4, 16384, 768], P('stage', 'data')
- loss_grad: bfloat16 [16384, 768], P('data')
- next_batch: bfloat16 [1, 16384, 768], P(None, 'data')
- learn_rate: float32 [], replicated
- max_norm: float32 [], replicated
Outputs:
- output 1: float32 [4, 768, 3072], P('stage')
- output 2: float32 [4, 3072, 768], P('stage')
- output 3: float32 [4, 768, 3072], P('stage')
- output 4: float32 [4, 3072, 768], P('stage')
- output 5: float32 [4, 768, 3072], P('stage')
- output 6: float32 [4, 3072, 768], P('stage')
- output 7: bfloat16 [4, 1, 16384, 768], P('stage', None, 'data')
All inputs are finite; a program needn't handle non-finite values.
Results may differ from a plain program's by a relative error of at most 0.00891411.
Values are sent between devices in bfloat16 or wider.
A program may use at most 1 GiB of HBM per device.

v0:
```python
import jax
import jax.numpy as jnp
from jax import lax
from jax.sharding import PartitionSpec as P

BETA1 = 0.9
BETA2 = 0.95
ADAM_EPS = 1e-8
WEIGHT_DECAY = 0.1
NORM_EPS = 1e-6
ADAM_STEP = 8
SQRT_TWO_PI = 0.7978845608028654
GELU_CUBIC = 0.044715


def tanh_part(pre_act):
    return jnp.tanh(SQRT_TWO_PI * (pre_act + GELU_CUBIC * pre_act * pre_act * pre_act))


def gelu_tanh(pre_act):
    return 0.5 * pre_act * (1.0 + tanh_part(pre_act))


def gelu_pair(pre_act):
    tanh_val = tanh_part(pre_act)
    act_value = 0.5 * pre_act * (1.0 + tanh_val)
    act_slope = 0.5 * (1.0 + tanh_val) + 0.5 * pre_act * (1.0 - tanh_val * tanh_val) * SQRT_TWO_PI * (1.0 + 3.0 * GELU_CUBIC * pre_act * pre_act)
    return act_value, act_slope


def mat_tn(left, right):
    return lax.dot_general(left, right, (((0,), (0,)), ((), ())), preferred_element_type=jnp.float32)


def mat_nt(left, right):
    return lax.dot_general(left, right, (((1,), (1,)), ((), ())), preferred_element_type=jnp.float32)


def adamw_update(master, first_mom, second_mom, grad_avg, clip_scale, learn_rate):
    scaled = clip_scale * grad_avg
    new_first = BETA1 * first_mom + (1.0 - BETA1) * scaled
    new_second = BETA2 * second_mom + (1.0 - BETA2) * scaled * scaled
    first_hat = new_first / (1.0 - BETA1 ** ADAM_STEP)
    second_hat = new_second / (1.0 - BETA2 ** ADAM_STEP)
    new_master = master - learn_rate * (first_hat / (jnp.sqrt(second_hat) + ADAM_EPS) + WEIGHT_DECAY * master)
    return new_master, new_first, new_second


def stage_forward(rows_in, up_bf, down_bf):
    pre_act = jnp.dot(rows_in, up_bf, preferred_element_type=jnp.float32)
    hidden = gelu_tanh(pre_act).astype(jnp.bfloat16)
    return (rows_in.astype(jnp.float32) + jnp.dot(hidden, down_bf, preferred_element_type=jnp.float32)).astype(jnp.bfloat16)


def solution(mesh):
    n_stages = mesh.shape['stage']
    n_reps = mesh.shape['data']
    last_stage = n_stages - 1
    down_pairs = [(source, source - 1) for source in range(1, n_stages)]
    up_pairs = [(source, source + 1) for source in range(n_stages - 1)]

    def local_step(master_up, master_down, mom1_up, mom1_down, mom2_up, mom2_down, grad_up, grad_down, stage_acts, loss_grad, next_batch, learn_rate, max_norm):
        stage_idx = lax.axis_index('stage')
        stage_in = stage_acts[0]
        up_bf = master_up[0].astype(jnp.bfloat16)
        down_bf = master_down[0].astype(jnp.bfloat16)
        tok_rows, model_width = stage_in.shape
        hidden_width = up_bf.shape[1]

        def local_back(grad_in):
            pre_act = jnp.dot(stage_in, up_bf, preferred_element_type=jnp.float32)
            act_value, act_slope = gelu_pair(pre_act)
            d_pre = (mat_nt(grad_in, down_bf) * act_slope).astype(jnp.bfloat16)
            return act_value.astype(jnp.bfloat16), d_pre

        def back_run(operands):
            grad_in = operands[0]
            hidden, d_pre = local_back(grad_in)
            d_rows = (grad_in.astype(jnp.float32) + mat_nt(d_pre, up_bf)).astype(jnp.bfloat16)
            return d_rows, grad_in, hidden, d_pre

        def back_skip(operands):
            return jnp.zeros_like(operands[0]), operands[1], operands[2], operands[3]

        def back_tick(step_idx, carry):
            received, grad_own, hid_own, dpre_own = carry
            grad_in = jnp.where(step_idx == 0, loss_grad, received)
            d_rows, grad_own, hid_own, dpre_own = lax.cond(stage_idx == last_stage - step_idx, back_run, back_skip, (grad_in, grad_own, hid_own, dpre_own))
            return lax.ppermute(d_rows, 'stage', down_pairs), grad_own, hid_own, dpre_own

        row_zeros = jnp.zeros((tok_rows, model_width), jnp.bfloat16)
        wide_zeros = jnp.zeros((tok_rows, hidden_width), jnp.bfloat16)
        received, grad_own, hid_own, dpre_own = lax.fori_loop(0, last_stage, back_tick, (row_zeros, row_zeros, wide_zeros, wide_zeros))

        def first_run(operands):
            hidden, d_pre = local_back(operands[0])
            return operands[0], hidden, d_pre

        def first_skip(operands):
            return operands[1], operands[2], operands[3]

        grad_own, hid_own, dpre_own = lax.cond(stage_idx == 0, first_run, first_skip, (received, grad_own, hid_own, dpre_own))

        gbar_up = lax.psum(grad_up[0, 0] + mat_tn(stage_in, dpre_own), 'data') / n_reps
        gbar_down = lax.psum(grad_down[0, 0] + mat_tn(hid_own, grad_own), 'data') / n_reps
        local_sq = jnp.sum(gbar_up * gbar_up) + jnp.sum(gbar_down * gbar_down)
        grad_norm = jnp.sqrt(lax.psum(local_sq, 'stage'))
        clip_scale = jnp.minimum(1.0, max_norm / (grad_norm + NORM_EPS))
        new_up, new_m1_up, new_m2_up = adamw_update(master_up[0], mom1_up[0], mom2_up[0], gbar_up, clip_scale, learn_rate)
        new_down, new_m1_down, new_m2_down = adamw_update(master_down[0], mom1_down[0], mom2_down[0], gbar_down, clip_scale, learn_rate)
        new_up_bf = new_up.astype(jnp.bfloat16)
        new_down_bf = new_down.astype(jnp.bfloat16)
        n_micro = next_batch.shape[0]
        n_ticks = n_micro + last_stage

        def fwd_compute(tick_idx, received, stage_outs):
            micro_idx = tick_idx - stage_idx
            safe_idx = jnp.clip(micro_idx, 0, n_micro - 1)
            first_in = lax.dynamic_index_in_dim(next_batch, safe_idx, 0, keepdims=False)
            rows_in = jnp.where(stage_idx == 0, first_in, received)

            def fwd_run(operands):
                rows_out = stage_forward(operands[0], new_up_bf, new_down_bf)
                return rows_out, lax.dynamic_update_index_in_dim(operands[1], rows_out, safe_idx, 0)

            def fwd_skip(operands):
                return jnp.zeros_like(operands[0]), operands[1]

            active = (micro_idx >= 0) & (micro_idx < n_micro)
            return lax.cond(active, fwd_run, fwd_skip, (rows_in, stage_outs))

        def fwd_tick(tick_idx, carry):
            rows_out, stage_outs = fwd_compute(tick_idx, carry[0], carry[1])
            return lax.ppermute(rows_out, 'stage', up_pairs), stage_outs

        outs_init = jnp.zeros((n_micro, tok_rows, model_width), jnp.bfloat16)
        received, stage_outs = lax.fori_loop(0, n_ticks - 1, fwd_tick, (row_zeros, outs_init))
        _, stage_outs = fwd_compute(n_ticks - 1, received, stage_outs)
        return (new_up[None], new_down[None], new_m1_up[None], new_m1_down[None], new_m2_up[None], new_m2_down[None], stage_outs[None])

    w_spec = P('stage', None, None)
    g_spec = P('data', 'stage', None, None)
    in_specs = (w_spec, w_spec, w_spec, w_spec, w_spec, w_spec, g_spec, g_spec, P('stage', 'data', None), P('data', None), P(None, 'data', None), P(), P())
    out_specs = (w_spec, w_spec, w_spec, w_spec, w_spec, w_spec, P('stage', None, 'data', None))
    return jax.shard_map(local_step, mesh=mesh, in_specs=in_specs, out_specs=out_specs, check_vma=False)
```

profile of v0, /device:TPU:3, one launch (start us, length us, event | category | flops | bytes accessed | tf_op | source)
XLA Modules:
  0.0 1255.3 jit_solution(12984066565276386313)
XLA Ops:
  7.2 9.6 copy.20
  16.8 6.3 bitcast_convert_fusion.1
  23.1 6.6 copy.23
  29.7 6.3 bitcast_convert_fusion
  36.1 6.2 broadcast_in_dim.38
  50.4 190.2 %while.41 = (s32[]{:T(128)}, bf16[2048,768]{1,0:T(8,128)(2,1)S(1)}, bf16[2048,768]{1,0:T(8,128)(2,1)}, bf16[2048,3072]{1,0:T(8,128)(2,1)}, bf16[2048,3072]{1,0:T...) while((s32[]{:T(128)}, bf16[2048,768]{1,0:T(8,128)(2,1)S(1)}, ...), condition=%wide.region_3.4_spmd, body=%wide.region_0.3_spmd.sunk | while | flops 29173481472 | bytes 187171152 | solution.py:93
  50.5 69.5 %conditional.8 = (bf16[2048,768]{1,0:T(8,128)(2,1)}, bf16[2048,768]{1,0:T(8,128)(2,1)}, bf16[2048,3072]{1,0:T(8,128)(2,1)}, bf16[2048,3072]{1,0:T(8,128)(2,1)}) conditional(s32[]{:T(128)} %convert_element_type.115, (bf16[2048,768]{1,0:T(8,128)(2,1)}, bf16[2048,3072]{1,0:T(8,128)(2,1)}, bf16[2048,3072]{1,0:T(8,128)(2,1)}) %tuple.120, (s32[]{:T(128)}, ...), branch_computations={%region_1.1_spmd, %region_2.2_spmd} | conditional | flops 29173481472 | bytes 174587968 | solution.py:88
  50.6 24.0 %multiply_convert_fusion = (bf16[2048,3072]{1,0:T(8,128)(2,1)}, f32[2048,3072]{1,0:T(8,128)}) fusion(bf16[2048,768]{1,0:T(8,128)(2,1)} %get-tuple-element.417, bf16[768,3072]{1,0:T(8,128)(2,1)} %get-tuple-element.418), kind=kOutput, calls=%fused_computation.9 | convolution fusion | flops 9720299520 | bytes 45613056 | tf_op jit(solution)/shard_map/while/body/eval_jaxpr/cond/branch_1_fun/dot_general | solution.py:71
  78.4 26.0 %fusion.6 = bf16[2048,3072]{1,0:T(8,128)(2,1)S(1)} fusion(f32[2048,3072]{1,0:T(8,128)} %get-tuple-element.561, bf16[2048,768]{1,0:T(8,128)(2,1)} %broadcast_select_fusion, bf16[3072,768]{1,0:T(8,128)(2,1)} %get-tuple-element.416), kind=kOutput, calls=%fused_computation.8 | convolution fusion | flops 9783214080 | bytes 45613056 | tf_op jit(solution)/shard_map/while/body/eval_jaxpr/cond/branch_1_fun/dot_general | solution.py:36
  104.4 15.6 %add_convert_fusion = bf16[2048,768]{1,0:T(8,128)(2,1)} fusion(bf16[2048,768]{1,0:T(8,128)(2,1)} %broadcast_select_fusion, bf16[2048,3072]{1,0:T(8,128)(2,1)S(1)} %fusion.6, bf16[768,3072]{1,0:T(8,128)(2,1)} %get-tuple-element.418), kind=kOutput, calls=%fused_computation.10 | convolution fusion | flops 9668395008 | bytes 23592960 | tf_op jit(solution)/shard_map/while/body/eval_jaxpr/cond/branch_1_fun/dot_general | solution.py:36
  128.4 68.1 %collective-permute-start = (bf16[2048,768]{1,0:T(8,128)(2,1)}, bf16[2048,768]{1,0:T(8,128)(2,1)S(1)}, u32[]{:S(2)}, u32[]{:S(2)}) collective-permute-start(bf16[2048,768]{1,0:T(8,128)(2,1)} %get-tuple-element.676), channel_id=1, source_target_pairs={{1,0},{2,1},{3,2},{5,4},{6,5},{7,6},{9,8},{10,9},{11,10},{13,12},{... | collective-permute-start | bytes 9437192 | tf_op jit(solution)/shard_map/while/body/eval_jaxpr/ppermute | solution.py:89
  203.5 31.6 %collective-permute-start = (bf16[2048,768]{1,0:T(8,128)(2,1)}, bf16[2048,768]{1,0:T(8,128)(2,1)S(1)}, u32[]{:S(2)}, u32[]{:S(2)}) collective-permute-start(bf16[2048,768]{1,0:T(8,128)(2,1)} %get-tuple-element.676), channel_id=1, source_target_pairs={{1,0},{2,1},{3,2},{5,4},{6,5},{7,6},{9,8},{10,9},{11,10},{13,12},{... | collective-permute-start | bytes 9437192 | tf_op jit(solution)/shard_map/while/body/eval_jaxpr/ppermute | solution.py:89
  240.6 9.6 copy.22
  250.1 17.9 %bitcast_add_fusion.2 = f32[768,3072]{0,1:T(8,128)} fusion(f32[1,1,768,3072]{2,3,1,0:T(8,128)} %copy.22, bf16[2048,3072]{1,0:T(8,128)(2,1)} %get-tuple-element.479, bf16[1,2048,768]{2,1,0:T(8,128)(2,1)} %bitcast.112), kind=kOutput, calls=%fused_computation.59 | convolution fusion | flops 9666035712 | bytes 34603008 | tf_op jit(solution)/shard_map/dot_general | solution.py:32
  268.0 14.7 %bitcast_add_fusion.1 = f32[3072,768]{1,0:T(8,128)} fusion(f32[1,1,3072,768]{3,2,1,0:T(8,128)} %param.32, bf16[2048,3072]{1,0:T(8,128)(2,1)S(1)} %copy-done.1, bf16[2048,768]{1,0:T(8,128)(2,1)S(1)} %copy-done.3), kind=kOutput, calls=%fused_computation.58 | convolution fusion | flops 9666035712 | bytes 34603008 | tf_op jit(solution)/shard_map/dot_general | solution.py:32
  284.0 9.6 copy.21
  293.6 10.0 copy.25
  303.6 659.8 %all-reduce.3.cloned.1.call-done = (f32[768,3072]{0,1:T(8,128)}, f32[3072,768]{1,0:T(8,128)}) async-done(((f32[768,3072]{0,1:T(8,128)}, f32[3072,768]{1,0:T(8,128)}), (f32[768,3072]{0,1:T(8,128)}, f32[3072,768]{1,0:T(8,128)})) %all-reduce.3.cloned.1.call-update) | async-done | bytes 18874384 | tf_op jit(solution)/shard_map/psum | solution.py:104
  963.3 6.9 multiply_reduce_fusion
  974.5 6.7 psum.23
  981.9 28.6 %fusion.63 = (bf16[768,3072]{0,1:T(8,128)(2,1)}, f32[768,3072]{0,1:T(8,128)}, f32[1,768,3072]{1,2,0:T(8,128)}, f32[1,768,3072]{1,2,0:T(8,128)}) fusion(f32[1,768,3072]{1,2,0:T(8,128)} %copy.25, f32[768,3072]{0,1:T(8,128)} %get-tuple-element.554, f32[]{:T(128)S(6)} %mul.252, f32[1,768,3072]{1,2,0:T(8,128)} %copy.21, f32[]{:T(128)S(6)} %copy.80, ...), kind=kLoop, calls=%fused_computation.79 | loop fusion | flops 40108032 | bytes 70778888 | tf_op jit(solution)/shard_map/convert_element_type | solution.py:111
  1010.5 6.6 copy.26
  1017.1 28.5 %fusion.62 = (bf16[3072,768]{1,0:T(8,128)(2,1)}, f32[3072,768]{1,0:T(8,128)}, f32[1,3072,768]{2,1,0:T(8,128)}, f32[1,3072,768]{2,1,0:T(8,128)}) fusion(f32[1,3072,768]{2,1,0:T(8,128)} %param.30, f32[3072,768]{1,0:T(8,128)} %get-tuple-element.555, f32[]{:T(128)S(6)} %mul.252, f32[1,3072,768]{2,1,0:T(8,128)} %param.28, f32[]{:T(128)S(6)} %copy.80, ...), kind=kLoop, calls=%fused_computation.78 | loop fusion | flops 40108032 | bytes 70778888 | tf_op jit(solution)/shard_map/convert_element_type | solution.py:112
  1047.8 145.2 %while.42 = (s32[]{:T(128)}, bf16[2048,768]{1,0:T(8,128)(2,1)S(1)}, bf16[1,2048,768]{2,1,0:T(8,128)(2,1)}, s32[]{:T(128)}, pred[]{:T(512)}, /*index=5*/bf16[1,20...) while((s32[]{:T(128)}, bf16[2048,768]{1,0:T(8,128)(2,1)S(1)}, ...), condition=%wide.region_14.15_spmd, body=%wide.region_11.14_spmd.sunk | while | flops 19391840256 | bytes 37748968 | solution.py:137
  1051.1 6.7 collective-permute-done.1
  1060.9 37.3 %collective-permute-done.1 = bf16[2048,768]{1,0:T(8,128)(2,1)S(1)} collective-permute-done((bf16[2048,768]{1,0:T(8,128)(2,1)}, bf16[2048,768]{1,0:T(8,128)(2,1)S(1)}, u32[]{:S(2)}, u32[]{:S(2)}) %collective-permute-start.1) | collective-permute-done | bytes 3145760 | tf_op jit(solution)/shard_map/while/body/eval_jaxpr/ppermute | solution.py:134
  1101.4 91.6 %collective-permute-done.1 = bf16[2048,768]{1,0:T(8,128)(2,1)S(1)} collective-permute-done((bf16[2048,768]{1,0:T(8,128)(2,1)}, bf16[2048,768]{1,0:T(8,128)(2,1)S(1)}, u32[]{:S(2)}, u32[]{:S(2)}) %collective-permute-start.1) | collective-permute-done | bytes 3145760 | tf_op jit(solution)/shard_map/while/body/eval_jaxpr/ppermute | solution.py:134
  1192.9 9.6 copy.28
  1202.5 9.6 copy.29
  1212.1 9.6 copy.30
  1221.7 26.6 %conditional.5 = (bf16[1,1,2048,768]{3,2,1,0:T(8,128)(2,1)}) conditional(s32[]{:T(128)} %convert_element_type.82, bf16[1,2048,768]{2,1,0:T(8,128)(2,1)} %get-tuple-element.482, (pred[]{:T(512)}, bf16[1,2048,768]{2,1,0:T(8,128)(2,1)}, bf16[2048,768]{1,0:T(8,128)(2,1)S(1)}, bf16[768,3072]{0,1:T(8,128)(2,1)}, bf16[3072,768]{1,0:T(8,128)(2,1)}) %tuple.147), branch_computations={%region_15.16_spmd, %region_16.17_spmd} | conditional | flops 19391840256 | bytes 18874376 | solution.py:130
  1221.7 26.6 %fusion.44 = bf16[1,1,2048,768]{3,2,1,0:T(8,128)(2,1)} fusion(bf16[3072,768]{1,0:T(8,128)(2,1)} %get-tuple-element.458, bf16[768,3072]{0,1:T(8,128)(2,1)} %get-tuple-element.509, bf16[2048,768]{1,0:T(8,128)(2,1)S(1)} %get-tuple-element.456, bf16[1,2048,768]{2,1,0:T(8,128)(2,1)} %get-tuple-element.455, pred[]{:T(512)} %get-tuple-element.454), kind=kOutput, calls=%fused_computation.48 | convolution fusion | flops 19391840256 | bytes 18874368 | tf_op jit(solution)/shard_map/cond/branch_1_fun/dot_general | solution.py:52
  (35 shorter events, 56.4 us)
Async XLA Ops:
  7.2 956.2 %all-reduce.3.cloned.1.call-start = ((), (), s32[]{:S(2)}) async-start(), calls=%async_computation | async-start | bytes 37748736 | tf_op jit(solution)/shard_map/psum | solution.py:104
  104.4 15.6 %copy-start.2 = (bf16[2048,3072]{1,0:T(8,128)(2,1)}, bf16[2048,3072]{1,0:T(8,128)(2,1)S(1)}, u32[]{:S(2)}) copy-start(bf16[2048,3072]{1,0:T(8,128)(2,1)S(1)} %fusion.6) | copy-start | bytes 37748740 | tf_op jit(solution)/shard_map/while/body/eval_jaxpr/cond
  120.0 6.6 collective-permute-start
  128.4 73.2 %collective-permute-start = (bf16[2048,768]{1,0:T(8,128)(2,1)}, bf16[2048,768]{1,0:T(8,128)(2,1)S(1)}, u32[]{:S(2)}, u32[]{:S(2)}) collective-permute-start(bf16[2048,768]{1,0:T(8,128)(2,1)} %get-tuple-element.676), channel_id=1, source_target_pairs={{1,0},{2,1},{3,2},{5,4},{6,5},{7,6},{9,8},{10,9},{11,10},{13,12},{... | collective-permute-start | bytes 9437192 | tf_op jit(solution)/shard_map/while/body/eval_jaxpr/ppermute | solution.py:89
  203.5 36.7 %collective-permute-start = (bf16[2048,768]{1,0:T(8,128)(2,1)}, bf16[2048,768]{1,0:T(8,128)(2,1)S(1)}, u32[]{:S(2)}, u32[]{:S(2)}) collective-permute-start(bf16[2048,768]{1,0:T(8,128)(2,1)} %get-tuple-element.676), channel_id=1, source_target_pairs={{1,0},{2,1},{3,2},{5,4},{6,5},{7,6},{9,8},{10,9},{11,10},{13,12},{... | collective-permute-start | bytes 9437192 | tf_op jit(solution)/shard_map/while/body/eval_jaxpr/ppermute | solution.py:89
  250.1 17.9 %copy-start.1 = (bf16[2048,3072]{1,0:T(8,128)(2,1)S(1)}, bf16[2048,3072]{1,0:T(8,128)(2,1)}, u32[]{:S(2)}) copy-start(bf16[2048,3072]{1,0:T(8,128)(2,1)} %get-tuple-element.480) | copy-start | bytes 37748740
  250.1 17.9 %copy-start.3 = (bf16[2048,768]{1,0:T(8,128)(2,1)S(1)}, bf16[2048,768]{1,0:T(8,128)(2,1)}, u32[]{:S(2)}) copy-start(bf16[2048,768]{1,0:T(8,128)(2,1)} %get-tuple-element.481) | copy-start | bytes 9437188
  963.3 6.9 copy-start
  1049.8 7.9 collective-permute-start.1
  1059.6 38.6 %collective-permute-start.1 = (bf16[2048,768]{1,0:T(8,128)(2,1)}, bf16[2048,768]{1,0:T(8,128)(2,1)S(1)}, u32[]{:S(2)}, u32[]{:S(2)}) collective-permute-start(bf16[2048,768]{1,0:T(8,128)(2,1)} %get-tuple-element.688), channel_id=1, source_target_pairs={{0,1},{1,2},{2,3},{4,5},{5,6},{6,7},{8,9},{9,10},{10,11},{12,13},{... | collective-permute-start | bytes 9437192 | tf_op jit(solution)/shard_map/while/body/eval_jaxpr/ppermute | solution.py:134
  1100.1 92.9 %collective-permute-start.1 = (bf16[2048,768]{1,0:T(8,128)(2,1)}, bf16[2048,768]{1,0:T(8,128)(2,1)S(1)}, u32[]{:S(2)}, u32[]{:S(2)}) collective-permute-start(bf16[2048,768]{1,0:T(8,128)(2,1)} %get-tuple-element.688), channel_id=1, source_target_pairs={{0,1},{1,2},{2,3},{4,5},{5,6},{6,7},{8,9},{9,10},{10,11},{12,13},{... | collective-permute-start | bytes 9437192 | tf_op jit(solution)/shard_map/while/body/eval_jaxpr/ppermute | solution.py:134
Sparse Core Ops, SparseCore 0:
  282.8 680.4 all-reduce.2
where the time goes:
time: 1260 us
  waiting for transfers between devices  810 us (64%)
  matrix products  125 us (10%)
  local copies, waits for them, and re-layouts  106 us (8%)
  starting transfers between devices  105 us (8%)
  other arithmetic  83.6 us (7%)
  between operations  17.6 us (1%)
    psum x1, waiting for transfers between devices, local_step(): lax.psum(grad_up[0, 0] + mat_tn(stage_in, dpre_own), 'data') / n_reps  660 us
    ppermute x3, waiting for transfers between devices, fwd_tick(): return (lax.ppermute(rows_out, 'stage', up_pairs), stage_outs)  136 us
    ppermute x3, starting transfers between devices, back_tick(): lax.ppermute(d_rows, 'stage', down_pairs)  101 us
    unnamed x13, local copies, waits for them, and re-layouts  67.5 us
    dot_general x2, matrix products, mat_nt(): lax.dot_general(left, right, (((1,), (1,)), ((), ())), preferred_element_...  41.6 us
    dot_general x2, matrix products, mat_tn(): lax.dot_general(left, right, (((0,), (0,)), ((), ())), preferred_element_...  32.5 us
    convert_element_type x1, other arithmetic, local_step(): new_up_bf = new_up.astype(jnp.bfloat16)  28.6 us
    convert_element_type x1, other arithmetic, local_step(): new_down_bf = new_down.astype(jnp.bfloat16)  28.5 us
  transfers between devices with their start and end apart: 7, of which 7 were waited for; matrix products, arithmetic and copies ran while one was open for 2% of the time, Pallas kernels for 0%

commit v1 on v0

v1 whole, which is shorter than its diff:
```python
import functools

import jax
import jax.numpy as jnp
from jax import lax
from jax.experimental import pallas as pl
from jax.experimental.pallas import tpu as pltpu
from jax.sharding import PartitionSpec as P

BETA1 = 0.9
BETA2 = 0.95
ADAM_EPS = 1e-8
WEIGHT_DECAY = 0.1
NORM_EPS = 1e-6
ADAM_STEP = 8
SQRT_TWO_PI = 0.7978845608028654
GELU_CUBIC = 0.044715
CHUNK = 256
TILE = 512
SUM_CHUNKS = 48
SUM_SKEW = 1
MESH = pl.DeviceIdType.MESH


def tanh_part(pre_act):
    return jnp.tanh(SQRT_TWO_PI * (pre_act + GELU_CUBIC * pre_act * pre_act * pre_act))


def gelu_tanh(pre_act):
    return 0.5 * pre_act * (1.0 + tanh_part(pre_act))


def gelu_pair(pre_act):
    tanh_val = tanh_part(pre_act)
    act_value = 0.5 * pre_act * (1.0 + tanh_val)
    act_slope = 0.5 * (1.0 + tanh_val) + 0.5 * pre_act * (1.0 - tanh_val * tanh_val) * SQRT_TWO_PI * (1.0 + 3.0 * GELU_CUBIC * pre_act * pre_act)
    return act_value, act_slope


def mat_tn(left, right):
    return lax.dot_general(left, right, (((0,), (0,)), ((), ())), preferred_element_type=jnp.float32)


def mat_nt(left, right):
    return lax.dot_general(left, right, (((1,), (1,)), ((), ())), preferred_element_type=jnp.float32)


def mat_nn(left, right):
    return lax.dot_general(left, right, (((1,), (0,)), ((), ())), preferred_element_type=jnp.float32)


def adamw_update(master, first_mom, second_mom, grad_avg, clip_scale, learn_rate):
    scaled = clip_scale * grad_avg
    new_first = BETA1 * first_mom + (1.0 - BETA1) * scaled
    new_second = BETA2 * second_mom + (1.0 - BETA2) * scaled * scaled
    first_hat = new_first / (1.0 - BETA1 ** ADAM_STEP)
    second_hat = new_second / (1.0 - BETA2 ** ADAM_STEP)
    new_master = master - learn_rate * (first_hat / (jnp.sqrt(second_hat) + ADAM_EPS) + WEIGHT_DECAY * master)
    return new_master, new_first, new_second


def enter(step, rep, stage, n_stages):
    @pl.when(step == 0)
    def _():
        barrier = pltpu.get_barrier_semaphore()

        @pl.when(stage > 0)
        def _():
            pl.semaphore_signal(barrier, inc=1, device_id=(rep, stage - 1), device_id_type=MESH)

        @pl.when(stage < n_stages - 1)
        def _():
            pl.semaphore_signal(barrier, inc=1, device_id=(rep, stage + 1), device_id_type=MESH)

        inner = (stage > 0) & (stage < n_stages - 1)

        @pl.when(inner)
        def _():
            pl.semaphore_wait(barrier, 2)

        @pl.when(jnp.logical_not(inner))
        def _():
            pl.semaphore_wait(barrier, 1)


def back_kernel(n_stages, n_chunks, tile, acts_ref, up_ref, down_ref, loss_ref, hid_ref, dpre_ref, gout_ref, gin, gsend, slope, send_sem, recv_sem):
    step = pl.program_id(0)
    rep = lax.axis_index('data')
    stage = lax.axis_index('stage')
    ff = up_ref.shape[1]
    enter(step, rep, stage, n_stages)

    def copy_of(idx):
        return pltpu.make_async_remote_copy(
            src_ref=gsend.at[idx],
            dst_ref=gin.at[idx],
            send_sem=send_sem.at[idx],
            recv_sem=recv_sem.at[idx],
            device_id=(rep, jnp.maximum(stage - 1, 0)),
            device_id_type=MESH,
        )

    rows_in = acts_ref[...]
    for start in range(0, ff, tile):
        cols = slice(start, start + tile)
        act_value, act_slope = gelu_pair(mat_nn(rows_in, up_ref[:, cols]))
        hid_ref[:, cols] = act_value.astype(jnp.bfloat16)
        slope[:, cols] = act_slope

    @pl.when(stage == n_stages - 1)
    def _():
        gin[step] = loss_ref[...]

    @pl.when(stage < n_stages - 1)
    def _():
        copy_of(step).wait_recv()

    grad_in = gin[step]
    gout_ref[...] = grad_in
    total = grad_in.astype(jnp.float32)
    back = jnp.zeros_like(total)
    for start in range(0, ff, tile):
        cols = slice(start, start + tile)
        d_pre = (mat_nt(grad_in, down_ref[cols, :]) * slope[:, cols]).astype(jnp.bfloat16)
        dpre_ref[:, cols] = d_pre
        back = back + mat_nt(d_pre, up_ref[:, cols])

    @pl.when(stage > 0)
    def _():
        gsend[step] = (total + back).astype(jnp.bfloat16)
        copy_of(step).start()

    @pl.when((step == n_chunks - 1) & (stage > 0))
    def _():
        for idx in range(n_chunks):
            copy_of(idx).wait_send()


def backward(n_stages, stage_in, up_bf, down_bf, loss_grad):
    rows, width = stage_in.shape
    ff = up_bf.shape[1]
    n_chunks = rows // CHUNK
    row_spec = pl.BlockSpec((CHUNK, width), lambda i: (i, 0))
    wide_spec = pl.BlockSpec((CHUNK, ff), lambda i: (i, 0))
    return pl.pallas_call(
        functools.partial(back_kernel, n_stages, n_chunks, TILE),
        grid=(n_chunks,),
        out_shape=(
            jax.ShapeDtypeStruct((rows, ff), jnp.bfloat16),
            jax.ShapeDtypeStruct((rows, ff), jnp.bfloat16),
            jax.ShapeDtypeStruct((rows, width), jnp.bfloat16),
        ),
        in_specs=[row_spec, pl.BlockSpec((width, ff), lambda i: (0, 0)), pl.BlockSpec((ff, width), lambda i: (0, 0)), row_spec],
        out_specs=(wide_spec, wide_spec, row_spec),
        scratch_shapes=[
            pltpu.VMEM((n_chunks, CHUNK, width), jnp.bfloat16),
            pltpu.VMEM((n_chunks, CHUNK, width), jnp.bfloat16),
            pltpu.VMEM((CHUNK, ff), jnp.float32),
            pltpu.SemaphoreType.DMA((n_chunks,)),
            pltpu.SemaphoreType.DMA((n_chunks,)),
        ],
        compiler_params=pltpu.CompilerParams(collective_id=0, has_side_effects=True, dimension_semantics=('arbitrary',), vmem_limit_bytes=60 * 2**20),
        name='backward',
    )(stage_in, up_bf, down_bf, loss_grad)


def fwd_kernel(n_stages, n_chunks, tile, first_ref, up_ref, down_ref, out_ref, xin, xsend, send_sem, recv_sem):
    step = pl.program_id(0)
    rep = lax.axis_index('data')
    stage = lax.axis_index('stage')
    ff = up_ref.shape[1]
    enter(step, rep, stage, n_stages)

    def copy_of(idx):
        return pltpu.make_async_remote_copy(
            src_ref=xsend.at[idx],
            dst_ref=xin.at[idx],
            send_sem=send_sem.at[idx],
            recv_sem=recv_sem.at[idx],
            device_id=(rep, jnp.minimum(stage + 1, n_stages - 1)),
            device_id_type=MESH,
        )

    @pl.when(stage == 0)
    def _():
        xin[step] = first_ref[...]

    @pl.when(stage > 0)
    def _():
        copy_of(step).wait_recv()

    rows_in = xin[step]
    total = jnp.zeros(rows_in.shape, jnp.float32)
    for start in range(0, ff, tile):
        cols = slice(start, start + tile)
        hidden = gelu_tanh(mat_nn(rows_in, up_ref[:, cols])).astype(jnp.bfloat16)
        total = total + mat_nn(hidden, down_ref[cols, :])
    rows_out = (rows_in.astype(jnp.float32) + total).astype(jnp.bfloat16)
    out_ref[...] = rows_out

    @pl.when(stage < n_stages - 1)
    def _():
        xsend[step] = rows_out
        copy_of(step).start()

    @pl.when((step == n_chunks - 1) & (stage < n_stages - 1))
    def _():
        for idx in range(n_chunks):
            copy_of(idx).wait_send()


def forward(n_stages, first_in, up_bf, down_bf):
    rows, width = first_in.shape
    ff = up_bf.shape[1]
    n_chunks = rows // CHUNK
    row_spec = pl.BlockSpec((CHUNK, width), lambda i: (i, 0))
    return pl.pallas_call(
        functools.partial(fwd_kernel, n_stages, n_chunks, TILE),
        grid=(n_chunks,),
        out_shape=jax.ShapeDtypeStruct((rows, width), jnp.bfloat16),
        in_specs=[row_spec, pl.BlockSpec((width, ff), lambda i: (0, 0)), pl.BlockSpec((ff, width), lambda i: (0, 0))],
        out_specs=row_spec,
        scratch_shapes=[
            pltpu.VMEM((n_chunks, CHUNK, width), jnp.bfloat16),
            pltpu.VMEM((n_chunks, CHUNK, width), jnp.bfloat16),
            pltpu.SemaphoreType.DMA((n_chunks,)),
            pltpu.SemaphoreType.DMA((n_chunks,)),
        ],
        compiler_params=pltpu.CompilerParams(collective_id=1, has_side_effects=True, dimension_semantics=('arbitrary',), vmem_limit_bytes=60 * 2**20),
        name='forward',
    )(first_in, up_bf, down_bf)


def sum_kernel(n_chunks, skew, up_ref, down_ref, out_up, out_down, y_up, z_up, x_up, z_down, x_down, y_down, send_sem, recv_sem, last_sem, local_sem):
    rep = lax.axis_index('data')
    stage = lax.axis_index('stage')
    z_pos = rep // 2
    y_pos = rep % 2
    inner = (z_pos == 1) | (z_pos == 2)
    outer = jnp.logical_not(inner)
    partner = rep + 1 - 2 * y_pos
    low = z_pos < 2
    near = jnp.where(low, 1 - z_pos, 5 - z_pos) * 2 + y_pos
    across = jnp.where(inner, 3 - z_pos, z_pos) * 2 + y_pos
    own_half = jnp.where(low, 0, 1)
    up_rows = up_ref.shape[0] // (2 * n_chunks)
    down_rows = down_ref.shape[0] // (2 * n_chunks)

    barrier = pltpu.get_barrier_semaphore()
    pl.semaphore_signal(barrier, inc=1, device_id=(partner, stage), device_id_type=MESH)
    pl.semaphore_signal(barrier, inc=1, device_id=(near, stage), device_id_type=MESH)

    @pl.when(inner)
    def _():
        pl.semaphore_signal(barrier, inc=1, device_id=(across, stage), device_id_type=MESH)
        pl.semaphore_wait(barrier, 3)

    @pl.when(outer)
    def _():
        pl.semaphore_wait(barrier, 2)

    def up_at(idx, half):
        return pl.ds(pl.multiple_of(idx * (2 * up_rows) + half * up_rows, up_rows), up_rows)

    def down_at(idx, half):
        return pl.ds(pl.multiple_of(idx * (2 * down_rows) + half * down_rows, down_rows), down_rows)

    def half_at(half):
        return pl.ds(pl.multiple_of(half * down_rows, down_rows), down_rows)

    def remote(src, dst, send, recv, peer):
        return pltpu.make_async_remote_copy(src_ref=src, dst_ref=dst, send_sem=send_sem.at[send], recv_sem=recv, device_id=(peer, stage), device_id_type=MESH)

    def raw_up(idx):
        return remote(up_ref.at[up_at(idx, 1 - y_pos)], y_up.at[idx], 0, recv_sem.at[0, idx], partner)

    def raw_down(idx):
        return remote(down_ref.at[pl.ds(pl.multiple_of(idx * (2 * down_rows), 2 * down_rows), 2 * down_rows)], z_down.at[idx], 1, recv_sem.at[1, idx], near)

    def pair_up(idx):
        return remote(y_up.at[idx], z_up.at[idx], 2, recv_sem.at[2, idx], near)

    def part_down(idx):
        return remote(z_down.at[idx, half_at(1 - own_half)], x_down.at[idx], 3, recv_sem.at[3, idx], across)

    def part_up(idx):
        return remote(z_up.at[idx], x_up.at[idx], 4, recv_sem.at[4, idx], across)

    def rail_down(idx):
        return remote(x_down.at[idx], y_down.at[idx], 5, recv_sem.at[5, idx], partner)

    def done_up_near(idx):
        return remote(x_up.at[idx], out_up.at[up_at(idx, y_pos)], 6, recv_sem.at[6, idx], near)

    def done_up_pair(idx):
        return remote(x_up.at[idx], out_up.at[up_at(idx, y_pos)], 7, last_sem.at[0], partner)

    def done_down_near(idx):
        return remote(y_down.at[idx], out_down.at[down_at(idx, own_half)], 8, last_sem.at[1], near)

    def done_down_across(idx):
        return remote(y_down.at[idx], out_down.at[down_at(idx, own_half)], 9, recv_sem.at[7, idx], across)

    def pass_up(idx):
        rows = up_at(idx, y_pos)
        return remote(out_up.at[rows], out_up.at[rows], 10, last_sem.at[0], partner)

    def pass_down(idx):
        rows = down_at(idx, 1 - own_half)
        return remote(out_down.at[rows], out_down.at[rows], 11, last_sem.at[1], near)

    def keep_up(idx):
        return pltpu.make_async_copy(x_up.at[idx], out_up.at[up_at(idx, y_pos)], local_sem.at[0])

    def keep_down(idx):
        return pltpu.make_async_copy(y_down.at[idx], out_down.at[down_at(idx, own_half)], local_sem.at[1])

    def valid(idx):
        return (idx >= 0) & (idx < n_chunks)

    def tick(step, carry):
        @pl.when(valid(step))
        def _():
            raw_up(step).start()

            @pl.when(outer)
            def _():
                raw_down(step).start()

        first = step - skew

        @pl.when(valid(first))
        def _():
            raw_up(first).wait_recv()
            y_up[first] = y_up[first] + up_ref[up_at(first, y_pos), :]

            @pl.when(outer)
            def _():
                pair_up(first).start()

            @pl.when(inner)
            def _():
                raw_down(first).wait_recv()
                z_down[first] = z_down[first] + down_ref[pl.ds(pl.multiple_of(first * (2 * down_rows), 2 * down_rows), 2 * down_rows), :]
                part_down(first).start()

        second = step - 2 * skew

        @pl.when(valid(second) & inner)
        def _():
            pair_up(second).wait_recv()
            z_up[second] = z_up[second] + y_up[second]
            part_up(second).start()
            part_down(second).wait_recv()
            x_down[second] = x_down[second] + z_down[second, half_at(own_half), :]
            rail_down(second).start()

        third = step - 3 * skew

        @pl.when(valid(third) & inner)
        def _():
            part_up(third).wait_recv()
            x_up[third] = x_up[third] + z_up[third]
            done_up_near(third).start()
            done_up_pair(third).start()
            keep_up(third).start()
            rail_down(third).wait_recv()
            y_down[third] = y_down[third] + x_down[third]
            done_down_across(third).start()
            done_down_near(third).start()
            keep_down(third).start()

        fourth = step - 4 * skew

        @pl.when(valid(fourth) & outer)
        def _():
            done_up_near(fourth).wait_recv()
            pass_up(fourth).start()

        @pl.when(valid(fourth) & inner)
        def _():
            remote(y_down.at[fourth], out_down.at[down_at(fourth, 1 - own_half)], 9, recv_sem.at[7, fourth], across).wait_recv()
            pass_down(fourth).start()

        return carry

    lax.fori_loop(0, n_chunks + 4 * skew, tick, 0)

    up_half = pl.ds(0, up_ref.shape[0] // 2)
    down_half = pl.ds(0, down_ref.shape[0] // 2)

    def all_up(send, recv, peer):
        return remote(up_ref.at[up_half], out_up.at[up_half], send, recv, peer)

    def all_down(send, recv, peer):
        return remote(down_ref.at[down_half], out_down.at[down_half], send, recv, peer)

    all_up(0, last_sem.at[0], partner).wait_send()
    all_up(0, last_sem.at[0], partner).wait_recv()

    @pl.when(outer)
    def _():
        remote(down_ref, out_down, 1, last_sem.at[1], near).wait_send()
        all_up(2, last_sem.at[0], near).wait_send()
        all_up(10, last_sem.at[0], partner).wait_send()
        remote(down_ref, out_down, 1, last_sem.at[1], near).wait_recv()

    @pl.when(inner)
    def _():
        all_down(3, last_sem.at[1], across).wait_send()
        all_up(4, last_sem.at[0], across).wait_send()
        all_down(5, last_sem.at[1], partner).wait_send()
        all_up(6, last_sem.at[0], near).wait_send()
        all_up(7, last_sem.at[0], partner).wait_send()
        all_down(8, last_sem.at[1], near).wait_send()
        all_down(9, last_sem.at[1], across).wait_send()
        all_down(11, last_sem.at[1], near).wait_send()
        pltpu.make_async_copy(up_ref.at[up_half], out_up.at[up_half], local_sem.at[0]).wait()
        pltpu.make_async_copy(down_ref.at[down_half], out_down.at[down_half], local_sem.at[1]).wait()


def sum_grads(grad_up, grad_down):
    n_up = grad_up.shape[0] // (2 * SUM_CHUNKS)
    n_down = grad_down.shape[0] // (2 * SUM_CHUNKS)
    up_land = pltpu.VMEM((SUM_CHUNKS, n_up, grad_up.shape[1]), jnp.float32)
    down_land = pltpu.VMEM((SUM_CHUNKS, n_down, grad_down.shape[1]), jnp.float32)
    return pl.pallas_call(
        functools.partial(sum_kernel, SUM_CHUNKS, SUM_SKEW),
        out_shape=(jax.ShapeDtypeStruct(grad_up.shape, jnp.float32), jax.ShapeDtypeStruct(grad_down.shape, jnp.float32)),
        in_specs=[pl.BlockSpec(memory_space=pltpu.VMEM)] * 2,
        out_specs=(pl.BlockSpec(memory_space=pl.ANY), pl.BlockSpec(memory_space=pl.ANY)),
        scratch_shapes=[
            up_land,
            up_land,
            up_land,
            pltpu.VMEM((SUM_CHUNKS, 2 * n_down, grad_down.shape[1]), jnp.float32),
            down_land,
            down_land,
            pltpu.SemaphoreType.DMA((12,)),
            pltpu.SemaphoreType.DMA((8, SUM_CHUNKS)),
            pltpu.SemaphoreType.DMA((2,)),
            pltpu.SemaphoreType.DMA((2,)),
        ],
        compiler_params=pltpu.CompilerParams(collective_id=2, has_side_effects=True, vmem_limit_bytes=60 * 2**20),
        name='sum_grads',
    )(grad_up, grad_down)


def solution(mesh):
    n_stages = mesh.shape['stage']
    n_reps = mesh.shape['data']

    def local_step(master_up, master_down, mom1_up, mom1_down, mom2_up, mom2_down, grad_up, grad_down, stage_acts, loss_grad, next_batch, learn_rate, max_norm):
        stage_in = stage_acts[0]
        up_bf = master_up[0].astype(jnp.bfloat16)
        down_bf = master_down[0].astype(jnp.bfloat16)
        hid_own, dpre_own, grad_own = backward(n_stages, stage_in, up_bf, down_bf, loss_grad)

        sum_up, sum_down = sum_grads(grad_up[0, 0] + mat_tn(stage_in, dpre_own), grad_down[0, 0] + mat_tn(hid_own, grad_own))
        gbar_up = sum_up / n_reps
        gbar_down = sum_down / n_reps
        local_sq = jnp.sum(gbar_up * gbar_up) + jnp.sum(gbar_down * gbar_down)
        grad_norm = jnp.sqrt(lax.psum(local_sq, 'stage'))
        clip_scale = jnp.minimum(1.0, max_norm / (grad_norm + NORM_EPS))
        new_up, new_m1_up, new_m2_up = adamw_update(master_up[0], mom1_up[0], mom2_up[0], gbar_up, clip_scale, learn_rate)
        new_down, new_m1_down, new_m2_down = adamw_update(master_down[0], mom1_down[0], mom2_down[0], gbar_down, clip_scale, learn_rate)
        stage_out = forward(n_stages, next_batch[0], new_up.astype(jnp.bfloat16), new_down.astype(jnp.bfloat16))
        return (new_up[None], new_down[None], new_m1_up[None], new_m1_down[None], new_m2_up[None], new_m2_down[None], stage_out[None, None])

    w_spec = P('stage', None, None)
    g_spec = P('data', 'stage', None, None)
    in_specs = (w_spec, w_spec, w_spec, w_spec, w_spec, w_spec, g_spec, g_spec, P('stage', 'data', None), P('data', None), P(None, 'data', None), P(), P())
    out_specs = (w_spec, w_spec, w_spec, w_spec, w_spec, w_spec, P('stage', None, 'data', None))
    return jax.shard_map(local_step, mesh=mesh, in_specs=in_specs, out_specs=out_specs, check_vma=False)
```

time: 1260 us -> 594 us (0.47)
  waiting for transfers between devices: 810 us -> 0 us
  Pallas kernels: 0 us -> 446 us
  starting transfers between devices: 105 us -> 0 us
  local copies, waits for them, and re-layouts: 106 us -> 4.89 us
  matrix products: 125 us -> 33.6 us
  blocking collectives: 6.66 us -> 29.2 us
  between operations: 17.6 us -> 4.06 us
    psum x1 -> x0, waiting for transfers between devices: 660 us -> none  [local_step(): lax.psum(grad_up[0, 0] + mat_tn(stage_in, dpre_own), 'data') / n_reps]
    pallas_call x0 -> x3, Pallas kernels: none -> 446 us  [the longest x1 328 us: sum_grads(): pl.pallas_call(functools.partial(sum_kernel, SUM_CHUNKS, SUM_SKEW), out_s...]
    ppermute x6 -> x0, waiting for transfers between devices: 151 us -> none  [the longest x3 136 us: fwd_tick(): return (lax.ppermute(rows_out, 'stage', up_pairs), stage_outs)]
    ppermute x6 -> x0, starting transfers between devices: 105 us -> none  [the longest x3 101 us: back_tick(): lax.ppermute(d_rows, 'stage', down_pairs)]
    dot_general x4 -> x0, matrix products: 92.1 us -> none  [the longest x2 41.6 us: mat_nt(): lax.dot_general(left, right, (((1,), (1,)), ((), ())), preferred_element_...]
    unnamed x13 -> x15, local copies, waits for them, and re-layouts: 67.5 us -> 4.89 us
    psum x1, blocking collectives: 6.66 us -> 29.2 us  [local_step(): grad_norm = jnp.sqrt(lax.psum(local_sq, 'stage'))]
    broadcast_in_dim x3 -> x0, local copies, waits for them, and re-layouts: 14.1 us -> none  [the longest x2 12.2 us: local_step(): wide_zeros = jnp.zeros((tok_rows, hidden_width), jnp.bfloat16)]
  transfers between devices with their start and end apart: 7 -> 0, of which waited for: 7 -> 0; matrix products, arithmetic and copies ran while one was open for 2% -> 0% of each run, Pallas kernels for 0% -> 0%
where the time goes in v1:
time: 594 us
  Pallas kernels  446 us (75%)
  other arithmetic  75.9 us (13%)
  matrix products  33.6 us (6%)
  blocking collectives  29.2 us (5%)
    pallas_call x1, Pallas kernels, sum_grads(): pl.pallas_call(functools.partial(sum_kernel, SUM_CHUNKS, SUM_SKEW), out_s...  328 us
    pallas_call x1, Pallas kernels, backward(): pl.pallas_call(functools.partial(back_kernel, n_stages, n_chunks, TILE),...  60 us
    pallas_call x1, Pallas kernels, forward(): pl.pallas_call(functools.partial(fwd_kernel, n_stages, n_chunks, TILE), g...  58 us
    dot_general x2, matrix products, mat_tn(): lax.dot_general(left, right, (((0,), (0,)), ((), ())), preferred_element_...  33.6 us
    convert_element_type x1, other arithmetic, local_step(): new_down.astype(jnp.bfloat16)  29.4 us
    psum x1, blocking collectives, local_step(): grad_norm = jnp.sqrt(lax.psum(local_sq, 'stage'))  29.2 us
    convert_element_type x1, other arithmetic, local_step(): new_up.astype(jnp.bfloat16)  26.9 us

profile of v1, /device:TPU:3, one launch (start us, length us, event | category | flops | bytes accessed | tf_op | source)
XLA Modules:
  0.0 593.8 jit_solution(2166966788589149380)
XLA Ops:
  1.9 0.0 copy-start
  1.9 7.0 %bitcast_convert_fusion.1.up_ref = bf16[768,3072]{1,0:T(8,128)(2,1)} fusion(f32[1,768,3072]{2,1,0:T(8,128)} %param.13), kind=kLoop, calls=%fused_computation.15 | loop fusion | flops 2359296 | bytes 14155776 | tf_op jit(solution)/shard_map/convert_element_type | solution.py:455
  8.9 1.1 copy-done
  10.0 2.6 bitcast_convert_fusion.down_ref
  12.6 0.0 copy-start.2
  12.6 60.0 %backward.1 = (bf16[2048,3072]{1,0:T(8,128)(2,1)}, bf16[2048,3072]{1,0:T(8,128)(2,1)}, bf16[2048,768]{1,0:T(8,128)(2,1)}) custom-call(bf16[2048,768]{1,0:T(8,128)(2,1)} %bitcast.79, bf16[768,3072]{1,0:T(8,128)(2,1)} %bitcast_convert_fusion.1.up_ref, bf16[3072,768]{1,0:T(8,128)(2,1)} %bitcast_convert_fusion.down_ref, bf16[2048,768]{1,0:T(8,128)(2,1)} %loss_ref.1), custom_call_target="tpu_custom_call" | custom-call | tf_op jit(solution)/shard_map/backward/pallas_call | solution.py:145
  72.7 0.0 copy-done.2
  72.7 0.0 copy-start.3
  72.7 16.7 %bitcast_add_fusion.2.up_ref = f32[768,3072]{1,0:T(8,128)} fusion(f32[1,1,768,3072]{3,2,1,0:T(8,128)} %param.19, bf16[2048,3072]{1,0:T(8,128)(2,1)} %get-tuple-element.12, bf16[1,2048,768]{2,1,0:T(8,128)(2,1)S(1)} %copy-done.2), kind=kOutput, calls=%fused_computation.6 | convolution fusion | flops 9666035712 | bytes 34603008 | tf_op jit(solution)/shard_map/dot_general | solution.py:41
  89.4 0.0 copy-done.3
  89.4 16.8 %bitcast_add_fusion.1.down_ref = f32[3072,768]{1,0:T(8,128)} fusion(f32[1,1,3072,768]{3,2,1,0:T(8,128)} %param.20, bf16[2048,3072]{1,0:T(8,128)(2,1)} %get-tuple-element.13, bf16[2048,768]{1,0:T(8,128)(2,1)S(1)} %copy-done.3), kind=kOutput, calls=%fused_computation.5 | convolution fusion | flops 9666035712 | bytes 34603008 | tf_op jit(solution)/shard_map/dot_general | solution.py:41
  106.3 328.2 %sum_grads.1 = (f32[768,3072]{1,0:T(8,128)}, f32[3072,768]{1,0:T(8,128)}) custom-call(f32[768,3072]{1,0:T(8,128)} %bitcast_add_fusion.2.up_ref, f32[3072,768]{1,0:T(8,128)} %bitcast_add_fusion.1.down_ref), custom_call_target="tpu_custom_call" | custom-call | tf_op jit(solution)/shard_map/sum_grads/pallas_call | solution.py:427
  434.5 0.0 copy-start.1
  434.5 6.9 %multiply_reduce_fusion = f32[]{:T(128)} fusion(f32[3072,768]{1,0:T(8,128)} %get-tuple-element.16), kind=kLoop, calls=%fused_computation.18 | loop fusion | flops 7077887 | bytes 9437188 | tf_op jit(solution)/shard_map/reduce_sum | solution.py:462
  441.3 0.0 copy-done.1
  441.3 0.0 slice-start
  441.3 3.0 multiply_reduce_fusion.1
  445.7 29.2 %psum.7 = f32[]{:T(128)} all-reduce(f32[]{:T(128)S(6)} %add.46), channel_id=1, replica_groups=mesh['data'=8,'stage'=4] {'stage'}, use_global_device_ids=true, to_apply=%region_2.0 | all-reduce | flops 1 | bytes 8 | tf_op jit(solution)/shard_map/psum | solution.py:463
  475.6 0.0 slice-start.1
  475.6 0.0 slice-start.2
  475.6 29.4 %fusion.11 = (bf16[3072,768]{1,0:T(8,128)(2,1)}, f32[3072,768]{1,0:T(8,128)}, f32[1,3072,768]{2,1,0:T(8,128)}, f32[1,3072,768]{2,1,0:T(8,128)}) fusion(f32[1,3072,768]{2,1,0:T(8,128)} %param.18, f32[3072,768]{1,0:T(8,128)} %get-tuple-element.16, f32[]{:T(128)S(6)} %mul.104, f32[1,3072,768]{2,1,0:T(8,128)} %param.16, f32[]{:T(128)S(6)} %copy.23, ...), kind=kLoop, calls=%fused_computation.25 | loop fusion | flops 40108032 | bytes 70778888 | tf_op jit(solution)/shard_map/convert_element_type | solution.py:467
  505.1 0.0 slice-done
  505.1 0.0 slice-done.1
  505.1 0.0 slice-done.2
  505.1 26.9 %fusion.12 = (bf16[768,3072]{1,0:T(8,128)(2,1)}, f32[768,3072]{1,0:T(8,128)}, f32[1,768,3072]{2,1,0:T(8,128)}, f32[1,768,3072]{2,1,0:T(8,128)}) fusion(f32[1,768,3072]{2,1,0:T(8,128)} %param.17, f32[768,3072]{1,0:T(8,128)} %get-tuple-element.15, f32[]{:T(128)S(6)} %mul.104, f32[1,768,3072]{2,1,0:T(8,128)} %param.15, f32[]{:T(128)S(6)} %copy.23, ...), kind=kLoop, calls=%fused_computation.26 | loop fusion | flops 40108032 | bytes 70778888 | tf_op jit(solution)/shard_map/convert_element_type | solution.py:467
  532.0 58.0 %forward.1 = bf16[2048,768]{1,0:T(8,128)(2,1)} custom-call(bf16[2048,768]{1,0:T(8,128)(2,1)} %bitcast.80, bf16[768,3072]{1,0:T(8,128)(2,1)} %get-tuple-element.19.up_ref, bf16[3072,768]{1,0:T(8,128)(2,1)} %get-tuple-element.17.down_ref), custom_call_target="tpu_custom_call" | custom-call | tf_op jit(solution)/shard_map/forward/pallas_call | solution.py:217
  590.0 3.8 copy.25
  (1 shorter events, 0.0 us)
Async XLA Ops:
  1.9 8.1 %copy-start = (f32[1,3072,768]{2,1,0:T(8,128)S(1)}, f32[1,3072,768]{2,1,0:T(8,128)}, u32[]{:S(2)}) copy-start(f32[1,3072,768]{2,1,0:T(8,128)} %param.14) | copy-start | bytes 28311556
  12.6 60.0 %copy-start.2 = (bf16[1,2048,768]{2,1,0:T(8,128)(2,1)S(1)}, bf16[1,2048,768]{2,1,0:T(8,128)(2,1)}, u32[]{:S(2)}) copy-start(bf16[1,2048,768]{2,1,0:T(8,128)(2,1)} %param.21) | copy-start | bytes 9437188
  72.7 16.8 %copy-start.3 = (bf16[2048,768]{1,0:T(8,128)(2,1)S(1)}, bf16[2048,768]{1,0:T(8,128)(2,1)}, u32[]{:S(2)}) copy-start(bf16[2048,768]{1,0:T(8,128)(2,1)} %get-tuple-element.14) | copy-start | bytes 9437188
  434.5 6.9 %copy-start.1 = (f32[768,3072]{1,0:T(8,128)S(1)}, f32[768,3072]{1,0:T(8,128)}, u32[]{:S(2)}) copy-start(f32[768,3072]{1,0:T(8,128)} %get-tuple-element.15) | copy-start | bytes 28311556
  441.3 63.7 %slice-start = ((s8[9437184]{0:T(1024)(128)(4,1)}), s8[1048576]{0:T(1024)(128)(4,1)S(1)}, s32[]{:S(2)}) async-start(s8[9437184]{0:T(1024)(128)(4,1)} %bitcast.74), calls=%async_computation | async-start | bytes 2097152
  475.6 29.5 %slice-start.1 = ((s8[9437184]{0:T(1024)(128)(4,1)}), s8[4194304]{0:T(1024)(128)(4,1)S(1)}, s32[]{:S(2)}) async-start(s8[9437184]{0:T(1024)(128)(4,1)} %bitcast.74), calls=%async_computation.1 | async-start | bytes 8388608
  475.6 29.5 %slice-start.2 = ((s8[9437184]{0:T(1024)(128)(4,1)}), s8[4194304]{0:T(1024)(128)(4,1)S(1)}, s32[]{:S(2)}) async-start(s8[9437184]{0:T(1024)(128)(4,1)} %bitcast.74), calls=%async_computation.2 | async-start | bytes 8388608

commit v2 on v1

v2 whole, which is shorter than its diff:
```python
import functools

import jax
import jax.numpy as jnp
from jax import lax
from jax.experimental import pallas as pl
from jax.experimental.pallas import tpu as pltpu
from jax.sharding import PartitionSpec as P

BETA1 = 0.9
BETA2 = 0.95
ADAM_EPS = 1e-8
WEIGHT_DECAY = 0.1
NORM_EPS = 1e-6
ADAM_STEP = 8
SQRT_TWO_PI = 0.7978845608028654
GELU_CUBIC = 0.044715
CHUNK = 256
TILE = 768
LANES = 128
ADAM_BLOCKS = 6
SUM_SKEW = 1
MESH = pl.DeviceIdType.MESH


def tanh_part(pre_act):
    return jnp.tanh(SQRT_TWO_PI * (pre_act + GELU_CUBIC * pre_act * pre_act * pre_act))


def gelu_tanh(pre_act):
    return 0.5 * pre_act * (1.0 + tanh_part(pre_act))


def gelu_pair(pre_act):
    tanh_val = tanh_part(pre_act)
    act_value = 0.5 * pre_act * (1.0 + tanh_val)
    act_slope = 0.5 * (1.0 + tanh_val) + 0.5 * pre_act * (1.0 - tanh_val * tanh_val) * SQRT_TWO_PI * (1.0 + 3.0 * GELU_CUBIC * pre_act * pre_act)
    return act_value, act_slope


def mat_tn(left, right):
    return lax.dot_general(left, right, (((0,), (0,)), ((), ())), preferred_element_type=jnp.float32)


def mat_nt(left, right):
    return lax.dot_general(left, right, (((1,), (1,)), ((), ())), preferred_element_type=jnp.float32)


def mat_nn(left, right):
    return lax.dot_general(left, right, (((1,), (0,)), ((), ())), preferred_element_type=jnp.float32)


def adamw_update(master, first_mom, second_mom, grad_avg, clip_scale, learn_rate):
    scaled = clip_scale * grad_avg
    new_first = BETA1 * first_mom + (1.0 - BETA1) * scaled
    new_second = BETA2 * second_mom + (1.0 - BETA2) * scaled * scaled
    first_hat = new_first * (1.0 / (1.0 - BETA1 ** ADAM_STEP))
    second_hat = new_second * (1.0 / (1.0 - BETA2 ** ADAM_STEP))
    new_master = master - learn_rate * (first_hat / (jnp.sqrt(second_hat) + ADAM_EPS) + WEIGHT_DECAY * master)
    return new_master, new_first, new_second


def enter(step, rep, stage, n_stages):
    @pl.when(step == 0)
    def _():
        barrier = pltpu.get_barrier_semaphore()

        @pl.when(stage > 0)
        def _():
            pl.semaphore_signal(barrier, inc=1, device_id=(rep, stage - 1), device_id_type=MESH)

        @pl.when(stage < n_stages - 1)
        def _():
            pl.semaphore_signal(barrier, inc=1, device_id=(rep, stage + 1), device_id_type=MESH)

        inner = (stage > 0) & (stage < n_stages - 1)

        @pl.when(inner)
        def _():
            pl.semaphore_wait(barrier, 2)

        @pl.when(jnp.logical_not(inner))
        def _():
            pl.semaphore_wait(barrier, 1)


def put_blocks(ref, start, value):
    for offset in range(0, value.shape[1], LANES):
        ref[(start + offset) // LANES] = value[:, offset : offset + LANES]


def round_rows(src_ref, dst_ref, rows):
    def body(idx, carry):
        block = pl.ds(pl.multiple_of(idx * rows, rows), rows)
        dst_ref[block, :] = src_ref[block, :].astype(jnp.bfloat16)
        return carry

    lax.fori_loop(0, src_ref.shape[0] // rows, body, 0)


def back_kernel(n_stages, n_chunks, tile, acts_ref, up_hbm, down_hbm, loss_ref, hid_ref, dpre_ref, gout_ref, flip_ref, up_ref, down_ref, gin, gsend, slope, send_sem, recv_sem):
    step = pl.program_id(0)
    rep = lax.axis_index('data')
    stage = lax.axis_index('stage')
    ff = up_ref.shape[1]
    enter(step, rep, stage, n_stages)

    def copy_of(idx):
        return pltpu.make_async_remote_copy(
            src_ref=gsend.at[idx],
            dst_ref=gin.at[idx],
            send_sem=send_sem.at[idx],
            recv_sem=recv_sem.at[idx],
            device_id=(rep, jnp.maximum(stage - 1, 0)),
            device_id_type=MESH,
        )

    def ahead(rows_in, cols):
        act_value, act_slope = gelu_pair(mat_nn(rows_in, up_ref[:, cols]))
        put_blocks(hid_ref, cols.start, act_value.astype(jnp.bfloat16))
        slope[:, cols] = act_slope

    @pl.when(step == 0)
    def _():
        round_rows(up_hbm, up_ref, 64)
        round_rows(down_hbm, down_ref, 256)
        rows_in = acts_ref[...]
        flip_ref[...] = rows_in.T
        for start in range(0, ff, tile):
            ahead(rows_in, slice(start, start + tile))

    @pl.when(step > 0)
    def _():
        idx = step - 1

        @pl.when(stage == n_stages - 1)
        def _():
            gin[idx] = loss_ref[...]

        @pl.when(stage < n_stages - 1)
        def _():
            copy_of(idx).wait_recv()

        grad_in = gin[idx]
        gout_ref[...] = grad_in
        rows_in = acts_ref[...]
        flip_ref[...] = rows_in.T
        back = jnp.zeros(grad_in.shape, jnp.float32)
        for start in range(0, ff, tile):
            cols = slice(start, start + tile)
            d_pre = (mat_nt(grad_in, down_ref[cols, :]) * slope[:, cols]).astype(jnp.bfloat16)
            put_blocks(dpre_ref, start, d_pre)
            back = back + mat_nt(d_pre, up_ref[:, cols])
            ahead(rows_in, cols)

        @pl.when(stage > 0)
        def _():
            gsend[idx] = (grad_in.astype(jnp.float32) + back).astype(jnp.bfloat16)
            copy_of(idx).start()

    @pl.when((step == n_chunks) & (stage > 0))
    def _():
        for idx in range(n_chunks):
            copy_of(idx).wait_send()


def backward(n_stages, stage_in, master_up, master_down, loss_grad):
    rows, width = stage_in.shape
    ff = master_up.shape[1]
    n_chunks = rows // CHUNK

    def now(i):
        return jnp.minimum(i, n_chunks - 1)

    def late(i):
        return jnp.maximum(i - 1, 0)

    return pl.pallas_call(
        functools.partial(back_kernel, n_stages, n_chunks, TILE),
        grid=(n_chunks + 1,),
        out_shape=(
            jax.ShapeDtypeStruct((ff // LANES, rows, LANES), jnp.bfloat16),
            jax.ShapeDtypeStruct((ff // LANES, rows, LANES), jnp.bfloat16),
            jax.ShapeDtypeStruct((rows, width), jnp.bfloat16),
            jax.ShapeDtypeStruct((width, rows), jnp.bfloat16),
        ),
        in_specs=[
            pl.BlockSpec((CHUNK, width), lambda i: (now(i), 0)),
            pl.BlockSpec(memory_space=pltpu.VMEM),
            pl.BlockSpec(memory_space=pltpu.VMEM),
            pl.BlockSpec((CHUNK, width), lambda i: (late(i), 0)),
        ],
        out_specs=(
            pl.BlockSpec((ff // LANES, CHUNK, LANES), lambda i: (0, now(i), 0)),
            pl.BlockSpec((ff // LANES, CHUNK, LANES), lambda i: (0, late(i), 0)),
            pl.BlockSpec((CHUNK, width), lambda i: (late(i), 0)),
            pl.BlockSpec((width, CHUNK), lambda i: (0, now(i))),
        ),
        scratch_shapes=[
            pltpu.VMEM((width, ff), jnp.bfloat16),
            pltpu.VMEM((ff, width), jnp.bfloat16),
            pltpu.VMEM((n_chunks, CHUNK, width), jnp.bfloat16),
            pltpu.VMEM((n_chunks, CHUNK, width), jnp.bfloat16),
            pltpu.VMEM((CHUNK, ff), jnp.float32),
            pltpu.SemaphoreType.DMA((n_chunks,)),
            pltpu.SemaphoreType.DMA((n_chunks,)),
        ],
        compiler_params=pltpu.CompilerParams(collective_id=0, has_side_effects=True, dimension_semantics=('arbitrary',), vmem_limit_bytes=67043328),
        name='backward',
    )(stage_in, master_up, master_down, loss_grad)


def fwd_kernel(n_stages, n_chunks, tile, first_ref, up_ref, down_ref, out_ref, xin, xsend, send_sem, recv_sem):
    step = pl.program_id(0)
    rep = lax.axis_index('data')
    stage = lax.axis_index('stage')
    ff = up_ref.shape[1]
    enter(step, rep, stage, n_stages)

    def copy_of(idx):
        return pltpu.make_async_remote_copy(
            src_ref=xsend.at[idx],
            dst_ref=xin.at[idx],
            send_sem=send_sem.at[idx],
            recv_sem=recv_sem.at[idx],
            device_id=(rep, jnp.minimum(stage + 1, n_stages - 1)),
            device_id_type=MESH,
        )

    @pl.when(stage == 0)
    def _():
        xin[step] = first_ref[...]

    @pl.when(stage > 0)
    def _():
        copy_of(step).wait_recv()

    rows_in = xin[step]
    total = jnp.zeros(rows_in.shape, jnp.float32)
    for start in range(0, ff, tile):
        cols = slice(start, start + tile)
        hidden = gelu_tanh(mat_nn(rows_in, up_ref[:, cols])).astype(jnp.bfloat16)
        total = total + mat_nn(hidden, down_ref[cols, :])
    rows_out = (rows_in.astype(jnp.float32) + total).astype(jnp.bfloat16)
    out_ref[...] = rows_out

    @pl.when(stage < n_stages - 1)
    def _():
        xsend[step] = rows_out
        copy_of(step).start()

    @pl.when((step == n_chunks - 1) & (stage < n_stages - 1))
    def _():
        for idx in range(n_chunks):
            copy_of(idx).wait_send()


def forward(n_stages, first_in, up_bf, down_bf):
    rows, width = first_in.shape
    ff = up_bf.shape[1]
    n_chunks = rows // CHUNK
    row_spec = pl.BlockSpec((CHUNK, width), lambda i: (i, 0))
    return pl.pallas_call(
        functools.partial(fwd_kernel, n_stages, n_chunks, TILE),
        grid=(n_chunks,),
        out_shape=jax.ShapeDtypeStruct((rows, width), jnp.bfloat16),
        in_specs=[row_spec, pl.BlockSpec((width, ff), lambda i: (0, 0)), pl.BlockSpec((ff, width), lambda i: (0, 0))],
        out_specs=row_spec,
        scratch_shapes=[
            pltpu.VMEM((n_chunks, CHUNK, width), jnp.bfloat16),
            pltpu.VMEM((n_chunks, CHUNK, width), jnp.bfloat16),
            pltpu.SemaphoreType.DMA((n_chunks,)),
            pltpu.SemaphoreType.DMA((n_chunks,)),
        ],
        compiler_params=pltpu.CompilerParams(collective_id=1, has_side_effects=True, dimension_semantics=('arbitrary',), vmem_limit_bytes=60 * 2**20),
        name='forward',
    )(first_in, up_bf, down_bf)


def fold_squares(value):
    total = jnp.zeros((8, LANES), jnp.float32)
    for row in range(0, value.shape[0], 8):
        for col in range(0, value.shape[1], LANES):
            part = value[row : row + 8, col : col + LANES]
            total = total + part * part
    return total


def sum_kernel(n_chunks, skew, n_reps, flip_ref, dpre_hbm, hid_hbm, gown_ref, gup_hbm, gdown_hbm, out_up, out_down, sq_ref, acc_up, acc_down, dpre_buf, hid_buf, y_up, z_up, x_up, z_down, x_down, y_down, send_sem, recv_sem, last_sem, local_sem, load_sem, grad_sem, sq_part, sq_land, sq_send, sq_recv):
    rep = lax.axis_index('data')
    stage = lax.axis_index('stage')
    z_pos = rep // 2
    y_pos = rep % 2
    inner = (z_pos == 1) | (z_pos == 2)
    outer = jnp.logical_not(inner)
    partner = rep + 1 - 2 * y_pos
    low = z_pos < 2
    near = jnp.where(low, 1 - z_pos, 5 - z_pos) * 2 + y_pos
    across = jnp.where(inner, 3 - z_pos, z_pos) * 2 + y_pos
    own_half = jnp.where(low, 0, 1)
    n_blocks = n_chunks // 2
    up_rows = out_up.shape[0] // 4
    down_rows = out_down.shape[0] // (2 * n_chunks)

    def load_dpre(block):
        slot = lax.rem(block, 2)
        return pltpu.make_async_copy(dpre_hbm.at[block], dpre_buf.at[slot], load_sem.at[0, slot])

    def load_hid(block):
        slot = lax.rem(block, 2)
        return pltpu.make_async_copy(hid_hbm.at[block], hid_buf.at[slot], load_sem.at[1, slot])

    def load_gup(block):
        return pltpu.make_async_copy(gup_hbm.at[:, pl.ds(pl.multiple_of(block * LANES, LANES), LANES)], acc_up.at[block], grad_sem.at[0, block])

    def load_gdown(block):
        return pltpu.make_async_copy(gdown_hbm.at[pl.ds(pl.multiple_of(block * LANES, LANES), LANES)], acc_down.at[block], grad_sem.at[1, block])

    def build(block):
        slot = lax.rem(block, 2)
        load_dpre(block).wait()
        load_gup(block).wait()
        acc_up[block] = acc_up[block] + mat_nn(flip_ref[...], dpre_buf[slot])
        load_hid(block).wait()
        load_gdown(block).wait()
        acc_down[block] = acc_down[block] + mat_tn(hid_buf[slot], gown_ref[...])

        @pl.when(block + 2 < n_blocks)
        def _():
            load_dpre(block + 2).start()
            load_hid(block + 2).start()

    for block in range(2):
        load_dpre(block).start()
        load_gup(block).start()
        load_hid(block).start()
        load_gdown(block).start()

    def load_rest(block, carry):
        load_gup(block).start()
        load_gdown(block).start()
        return carry

    lax.fori_loop(2, n_blocks, load_rest, 0)
    sq_part[...] = jnp.zeros_like(sq_part)
    build(0)

    barrier = pltpu.get_barrier_semaphore()
    for hop in range(1, n_reps):
        pl.semaphore_signal(barrier, inc=1, device_id=(lax.rem(rep + hop, n_reps), stage), device_id_type=MESH)
    pl.semaphore_wait(barrier, n_reps - 1)

    def rows_at(idx, half):
        return pl.ds(pl.multiple_of((half * 2 + lax.rem(idx, 2)) * up_rows, up_rows), up_rows)

    def up_out(idx, half):
        return out_up.at[rows_at(idx, half), pl.ds(pl.multiple_of((idx // 2) * LANES, LANES), LANES)]

    def pair_at(idx):
        return pl.ds(pl.multiple_of(lax.rem(idx, 2) * (2 * down_rows), 2 * down_rows), 2 * down_rows)

    def down_at(idx, half):
        return pl.ds(pl.multiple_of(idx * (2 * down_rows) + half * down_rows, down_rows), down_rows)

    def half_at(half):
        return pl.ds(pl.multiple_of(half * down_rows, down_rows), down_rows)

    def remote(src, dst, send, recv, peer):
        return pltpu.make_async_remote_copy(src_ref=src, dst_ref=dst, send_sem=send_sem.at[send], recv_sem=recv, device_id=(peer, stage), device_id_type=MESH)

    def raw_up(idx):
        return remote(acc_up.at[idx // 2, rows_at(idx, 1 - y_pos)], y_up.at[idx], 0, recv_sem.at[0, idx], partner)

    def raw_down(idx):
        return remote(acc_down.at[idx // 2, pair_at(idx)], z_down.at[idx], 1, recv_sem.at[1, idx], near)

    def pair_up(idx):
        return remote(y_up.at[idx], z_up.at[idx], 2, recv_sem.at[2, idx], near)

    def part_down(idx):
        return remote(z_down.at[idx, half_at(1 - own_half)], x_down.at[idx], 3, recv_sem.at[3, idx], across)

    def part_up(idx):
        return remote(z_up.at[idx], x_up.at[idx], 4, recv_sem.at[4, idx], across)

    def rail_down(idx):
        return remote(x_down.at[idx], y_down.at[idx], 5, recv_sem.at[5, idx], partner)

    def done_up_near(idx):
        return remote(x_up.at[idx], up_out(idx, y_pos), 6, recv_sem.at[6, idx], near)

    def done_up_pair(idx):
        return remote(x_up.at[idx], up_out(idx, y_pos), 7, last_sem.at[0], partner)

    def done_down_near(idx):
        return remote(y_down.at[idx], out_down.at[down_at(idx, own_half)], 8, last_sem.at[1], near)

    def done_down_across(idx):
        return remote(y_down.at[idx], out_down.at[down_at(idx, own_half)], 9, recv_sem.at[7, idx], across)

    def pass_up(idx):
        return remote(up_out(idx, y_pos), up_out(idx, y_pos), 10, last_sem.at[0], partner)

    def pass_down(idx):
        rows = down_at(idx, 1 - own_half)
        return remote(out_down.at[rows], out_down.at[rows], 11, last_sem.at[1], near)

    def keep_up(idx):
        return pltpu.make_async_copy(x_up.at[idx], up_out(idx, y_pos), local_sem.at[0])

    def keep_down(idx):
        return pltpu.make_async_copy(y_down.at[idx], out_down.at[down_at(idx, own_half)], local_sem.at[1])

    def valid(idx):
        return (idx >= 0) & (idx < n_chunks)

    def tick(step, carry):
        @pl.when(valid(step))
        def _():
            raw_up(step).start()

            @pl.when(outer)
            def _():
                raw_down(step).start()

        first = step - skew

        @pl.when(valid(first))
        def _():
            raw_up(first).wait_recv()
            y_up[first] = y_up[first] + acc_up[first // 2, rows_at(first, y_pos), :]

            @pl.when(outer)
            def _():
                pair_up(first).start()

            @pl.when(inner)
            def _():
                raw_down(first).wait_recv()
                z_down[first] = z_down[first] + acc_down[first // 2, pair_at(first), :]
                part_down(first).start()

        second = step - 2 * skew

        @pl.when(valid(second) & inner)
        def _():
            pair_up(second).wait_recv()
            z_up[second] = z_up[second] + y_up[second]
            part_up(second).start()
            part_down(second).wait_recv()
            x_down[second] = x_down[second] + z_down[second, half_at(own_half), :]
            rail_down(second).start()

        third = step - 3 * skew

        @pl.when(valid(third) & inner)
        def _():
            part_up(third).wait_recv()
            total_up = x_up[third] + z_up[third]
            x_up[third] = total_up
            sq_part[0] = sq_part[0] + fold_squares(total_up / n_reps)
            done_up_near(third).start()
            done_up_pair(third).start()
            keep_up(third).start()
            rail_down(third).wait_recv()
            total_down = y_down[third] + x_down[third]
            y_down[third] = total_down
            sq_part[1] = sq_part[1] + fold_squares(total_down / n_reps)
            done_down_across(third).start()
            done_down_near(third).start()
            keep_down(third).start()

        fourth = step - 4 * skew

        @pl.when(valid(fourth) & outer)
        def _():
            done_up_near(fourth).wait_recv()
            pass_up(fourth).start()

        @pl.when(valid(fourth) & inner)
        def _():
            remote(y_down.at[fourth], out_down.at[down_at(fourth, 1 - own_half)], 9, recv_sem.at[7, fourth], across).wait_recv()
            pass_down(fourth).start()

        @pl.when((lax.rem(step, 2) == 1) & (step + 1 < n_chunks))
        def _():
            build((step + 1) // 2)

        return carry

    lax.fori_loop(0, n_chunks + 4 * skew, tick, 0)

    slot = jnp.where(low, 0, 2) + y_pos

    def square_copy(hop, source):
        return pltpu.make_async_remote_copy(src_ref=sq_land.at[source], dst_ref=sq_land.at[source], send_sem=sq_send.at[hop - 1], recv_sem=sq_recv.at[source], device_id=(lax.rem(rep + hop, n_reps), stage), device_id_type=MESH)

    @pl.when(inner)
    def _():
        sq_land[slot] = jnp.where(z_pos == 1, sq_part[0], 0.0) + jnp.where(y_pos == 0, sq_part[1], 0.0)
        for hop in range(1, n_reps):
            square_copy(hop, slot).start()

    up_half = pl.ds(0, out_up.shape[0] // 2)
    down_half = pl.ds(0, out_down.shape[0] // 2)

    def all_up(send, recv, peer):
        return remote(out_up.at[up_half], out_up.at[up_half], send, recv, peer)

    def all_down(send, recv, peer):
        return remote(out_down.at[down_half], out_down.at[down_half], send, recv, peer)

    all_up(0, last_sem.at[0], partner).wait_send()
    all_up(0, last_sem.at[0], partner).wait_recv()

    @pl.when(outer)
    def _():
        remote(out_down, out_down, 1, last_sem.at[1], near).wait_send()
        all_up(2, last_sem.at[0], near).wait_send()
        all_up(10, last_sem.at[0], partner).wait_send()
        remote(out_down, out_down, 1, last_sem.at[1], near).wait_recv()

    @pl.when(inner)
    def _():
        all_down(3, last_sem.at[1], across).wait_send()
        all_up(4, last_sem.at[0], across).wait_send()
        all_down(5, last_sem.at[1], partner).wait_send()
        all_up(6, last_sem.at[0], near).wait_send()
        all_up(7, last_sem.at[0], partner).wait_send()
        all_down(8, last_sem.at[1], near).wait_send()
        all_down(9, last_sem.at[1], across).wait_send()
        all_down(11, last_sem.at[1], near).wait_send()
        pltpu.make_async_copy(out_up.at[up_half], out_up.at[up_half], local_sem.at[0]).wait()
        pltpu.make_async_copy(out_down.at[down_half], out_down.at[down_half], local_sem.at[1]).wait()

    for source in range(4):
        @pl.when(rep != source + 2)
        def _():
            square_copy(1, source).wait_recv()

    @pl.when(inner)
    def _():
        for hop in range(1, n_reps):
            square_copy(hop, slot).wait_send()

    sq_ref[...] = sq_land[0] + sq_land[1] + sq_land[2] + sq_land[3]


def sum_grads(n_reps, flipped, dpre_own, hid_own, grad_own, grad_up, grad_down):
    width, ff = grad_up.shape
    rows = grad_own.shape[0]
    n_blocks = ff // LANES
    n_chunks = 2 * n_blocks
    up_land = pltpu.VMEM((n_chunks, width // 4, LANES), jnp.float32)
    down_land = pltpu.VMEM((n_chunks, LANES // 4, width), jnp.float32)
    vmem = pl.BlockSpec(memory_space=pltpu.VMEM)
    hbm = pl.BlockSpec(memory_space=pl.ANY)
    return pl.pallas_call(
        functools.partial(sum_kernel, n_chunks, SUM_SKEW, n_reps),
        out_shape=(jax.ShapeDtypeStruct(grad_up.shape, jnp.float32), jax.ShapeDtypeStruct(grad_down.shape, jnp.float32), jax.ShapeDtypeStruct((8, LANES), jnp.float32)),
        in_specs=[vmem, hbm, hbm, vmem, hbm, hbm],
        out_specs=(hbm, hbm, vmem),
        scratch_shapes=[
            pltpu.VMEM((n_blocks, width, LANES), jnp.float32),
            pltpu.VMEM((n_blocks, LANES, width), jnp.float32),
            pltpu.VMEM((2, rows, LANES), jnp.bfloat16),
            pltpu.VMEM((2, rows, LANES), jnp.bfloat16),
            up_land,
            up_land,
            up_land,
            pltpu.VMEM((n_chunks, LANES // 2, width), jnp.float32),
            down_land,
            down_land,
            pltpu.SemaphoreType.DMA((12,)),
            pltpu.SemaphoreType.DMA((8, n_chunks)),
            pltpu.SemaphoreType.DMA((2,)),
            pltpu.SemaphoreType.DMA((2,)),
            pltpu.SemaphoreType.DMA((2, 2)),
            pltpu.SemaphoreType.DMA((2, n_blocks)),
            pltpu.VMEM((2, 8, LANES), jnp.float32),
            pltpu.VMEM((4, 8, LANES), jnp.float32),
            pltpu.SemaphoreType.DMA((n_reps - 1,)),
            pltpu.SemaphoreType.DMA((4,)),
        ],
        compiler_params=pltpu.CompilerParams(collective_id=2, has_side_effects=True, vmem_limit_bytes=67043328),
        name='sum_grads',
    )(flipped, dpre_own, hid_own, grad_own, grad_up, grad_down)


def adam_kernel(n_reps, scale_ref, master_ref, first_ref, second_ref, sum_ref, new_master, new_first, new_second, new_bf):
    result, first_mom, second_mom = adamw_update(master_ref[...], first_ref[...], second_ref[...], sum_ref[...] / n_reps, scale_ref[0], scale_ref[1])
    new_master[...] = result
    new_first[...] = first_mom
    new_second[...] = second_mom
    new_bf[...] = result.astype(jnp.bfloat16)


def adam(n_reps, scales, master, first_mom, second_mom, grad_sum):
    rows, cols = master.shape
    block = pl.BlockSpec((rows // ADAM_BLOCKS, cols), lambda i: (i, 0))
    full = jax.ShapeDtypeStruct(master.shape, jnp.float32)
    return pl.pallas_call(
        functools.partial(adam_kernel, n_reps),
        grid=(ADAM_BLOCKS,),
        out_shape=(full, full, full, jax.ShapeDtypeStruct(master.shape, jnp.bfloat16)),
        in_specs=[pl.BlockSpec(memory_space=pltpu.SMEM), block, block, block, block],
        out_specs=(block, block, block, block),
        compiler_params=pltpu.CompilerParams(dimension_semantics=('arbitrary',), vmem_limit_bytes=60 * 2**20),
        name='adam',
    )(scales, master, first_mom, second_mom, grad_sum)


def solution(mesh):
    n_stages = mesh.shape['stage']
    n_reps = mesh.shape['data']

    def local_step(master_up, master_down, mom1_up, mom1_down, mom2_up, mom2_down, grad_up, grad_down, stage_acts, loss_grad, next_batch, learn_rate, max_norm):
        stage_in = stage_acts[0]
        hid_own, dpre_own, grad_own, flipped = backward(n_stages, stage_in, master_up[0], master_down[0], loss_grad)
        sum_up, sum_down, squares = sum_grads(n_reps, flipped, dpre_own, hid_own, grad_own, grad_up[0, 0], grad_down[0, 0])
        grad_norm = jnp.sqrt(lax.psum(jnp.sum(squares), 'stage'))
        clip_scale = jnp.minimum(1.0, max_norm / (grad_norm + NORM_EPS))
        scales = jnp.stack([clip_scale, learn_rate])
        new_up, new_m1_up, new_m2_up, up_bf = adam(n_reps, scales, master_up[0], mom1_up[0], mom2_up[0], sum_up)
        new_down, new_m1_down, new_m2_down, down_bf = adam(n_reps, scales, master_down[0], mom1_down[0], mom2_down[0], sum_down)
        stage_out = forward(n_stages, next_batch[0], up_bf, down_bf)
        return (new_up[None], new_down[None], new_m1_up[None], new_m1_down[None], new_m2_up[None], new_m2_down[None], stage_out[None, None])

    w_spec = P('stage', None, None)
    g_spec = P('data', 'stage', None, None)
    in_specs = (w_spec, w_spec, w_spec, w_spec, w_spec, w_spec, g_spec, g_spec, P('stage', 'data', None), P('data', None), P(None, 'data', None), P(), P())
    out_specs = (w_spec, w_spec, w_spec, w_spec, w_spec, w_spec, P('stage', None, 'data', None))
    return jax.shard_map(local_step, mesh=mesh, in_specs=in_specs, out_specs=out_specs, check_vma=False)
```

time: 594 us -> 532 us (0.90)
  other arithmetic: 75.9 us -> 1.93 us
  Pallas kernels: 446 us -> 487 us
  matrix products: 33.6 us -> 0 us
  blocking collectives: 29.2 us -> 36 us
    convert_element_type x4 -> x0, other arithmetic: 66 us -> none  [the longest x1 29.4 us: local_step(): new_down.astype(jnp.bfloat16)]
    pallas_call x1 -> x3, Pallas kernels: 328 us -> 377 us  [the longest x1 328 us: sum_grads(): pl.pallas_call(functools.partial(sum_kernel, n_chunks, SUM_SKEW, n_reps),...]
    dot_general x2 -> x0, matrix products: 33.6 us -> none  [mat_tn(): lax.dot_general(left, right, (((0,), (0,)), ((), ())), preferred_element_...]
    reduce_sum x2 -> x1, other arithmetic: 9.89 us -> 1.29 us  [local_step(): grad_norm = jnp.sqrt(lax.psum(jnp.sum(squares), 'stage'))]
    psum x1, blocking collectives: 29.2 us -> 36 us  [local_step(): grad_norm = jnp.sqrt(lax.psum(jnp.sum(squares), 'stage'))]
where the time goes in v2:
time: 532 us
  Pallas kernels  487 us (92%)
  blocking collectives  36 us (7%)
    pallas_call x1, Pallas kernels, sum_grads(): pl.pallas_call(functools.partial(sum_kernel, n_chunks, SUM_SKEW, n_reps),...  328 us
    pallas_call x1, Pallas kernels, forward(): pl.pallas_call(functools.partial(fwd_kernel, n_stages, n_chunks, TILE), g...  56.6 us
    pallas_call x1, Pallas kernels, backward(): pl.pallas_call(functools.partial(back_kernel, n_stages, n_chunks, TILE),...  54.1 us
    pallas_call x2, Pallas kernels, adam(): pl.pallas_call(functools.partial(adam_kernel, n_reps), grid=(ADAM_BLOCKS,...  48.4 us
    psum x1, blocking collectives, local_step(): grad_norm = jnp.sqrt(lax.psum(jnp.sum(squares), 'stage'))  36 us

profile of v2, /device:TPU:3, one launch (start us, length us, event | category | flops | bytes accessed | tf_op | source)
XLA Modules:
  0.0 531.6 jit_solution(42560146067438427)
XLA Ops:
  1.9 54.1 %backward.1 = (bf16[24,2048,128]{2,1,0:T(8,128)(2,1)}, bf16[24,2048,128]{2,1,0:T(8,128)(2,1)}, bf16[2048,768]{1,0:T(8,128)(2,1)}, bf16[768,2048]{1,0:T(8,128)(2,1)}) custom-call(bf16[2048,768]{1,0:T(8,128)(2,1)} %bitcast.31, f32[768,3072]{1,0:T(8,128)} %bitcast.22, f32[3072,768]{1,0:T(8,128)} %bitcast.20, bf16[2048,768]{1,0:T(8,128)(2,1)} %loss_ref.1), custom_call_target="tpu_custom_call" | custom-call | tf_op jit(solution)/shard_map/backward/pallas_call | solution.py:178
  56.0 328.1 %sum_grads.1 = (f32[768,3072]{1,0:T(8,128)}, f32[3072,768]{1,0:T(8,128)}, f32[8,128]{1,0:T(8,128)}) custom-call(bf16[768,2048]{1,0:T(8,128)(2,1)} %get-tuple-element.22.flip_ref, bf16[24,2048,128]{2,1,0:T(8,128)(2,1)} %get-tuple-element.23.dpre_hbm, bf16[24,2048,128]{2,1,0:T(8,128)(2,1)} %get-tuple-element.24.hid_hbm, ...), custom_call_target="tpu_custom_call" | custom-call | tf_op jit(solution)/shard_map/sum_grads/pallas_call | solution.py:558
  384.2 1.3 reduce_sum.9
  385.4 36.0 %psum.7 = f32[]{:T(128)} all-reduce(f32[]{:T(128)} %reduce_sum.9), channel_id=1, replica_groups=mesh['data'=8,'stage'=4] {'stage'}, use_global_device_ids=true, to_apply=%region_1.0 | all-reduce | flops 1 | bytes 8 | tf_op jit(solution)/shard_map/psum | solution.py:621
  422.2 0.6 pad_maximum_fusion.scale_ref
  422.8 24.2 %adam.3 = (f32[3072,768]{1,0:T(8,128)}, f32[3072,768]{1,0:T(8,128)}, f32[3072,768]{1,0:T(8,128)}, bf16[3072,768]{1,0:T(8,128)(2,1)}) custom-call(f32[2]{0:T(128)} %pad_maximum_fusion.scale_ref, f32[3072,768]{1,0:T(8,128)} %bitcast.21, f32[3072,768]{1,0:T(8,128)} %bitcast.25, f32[3072,768]{1,0:T(8,128)} %bitcast.26, f32[3072,768]{1,0:T(8,128)} %get-tuple-element.29.sum_ref), custom_call_target="tpu_custom_call" | custom-call | tf_op jit(solution)/shard_map/adam/pallas_call | solution.py:602
  447.0 24.3 %adam.2 = (f32[768,3072]{1,0:T(8,128)}, f32[768,3072]{1,0:T(8,128)}, f32[768,3072]{1,0:T(8,128)}, bf16[768,3072]{1,0:T(8,128)(2,1)}) custom-call(f32[2]{0:T(128)} %pad_maximum_fusion.scale_ref, f32[768,3072]{1,0:T(8,128)} %bitcast.23, f32[768,3072]{1,0:T(8,128)} %bitcast.27, f32[768,3072]{1,0:T(8,128)} %bitcast.28, f32[768,3072]{1,0:T(8,128)} %get-tuple-element.27.sum_ref), custom_call_target="tpu_custom_call" | custom-call | tf_op jit(solution)/shard_map/adam/pallas_call | solution.py:602
  471.2 56.6 %forward.1 = bf16[2048,768]{1,0:T(8,128)(2,1)} custom-call(bf16[2048,768]{1,0:T(8,128)(2,1)} %bitcast.32, bf16[768,3072]{1,0:T(8,128)(2,1)} %get-tuple-element.35.up_ref, bf16[3072,768]{1,0:T(8,128)(2,1)} %get-tuple-element.36.down_ref), custom_call_target="tpu_custom_call" | custom-call | tf_op jit(solution)/shard_map/forward/pallas_call | solution.py:263
  527.8 3.8 copy.23

commit v3 on v2

--- a/solution.py
+++ b/solution.py
@@ -18,7 +18,9 @@
 CHUNK = 256
 TILE = 768
 LANES = 128
-ADAM_BLOCKS = 6
+ADAM_BLOCKS = 8
+FWD_CHUNK = 128
+FWD_TILE = 1536
 SUM_SKEW = 1
 MESH = pl.DeviceIdType.MESH
 
@@ -258,17 +260,17 @@
 def forward(n_stages, first_in, up_bf, down_bf):
     rows, width = first_in.shape
     ff = up_bf.shape[1]
-    n_chunks = rows // CHUNK
-    row_spec = pl.BlockSpec((CHUNK, width), lambda i: (i, 0))
+    n_chunks = rows // FWD_CHUNK
+    row_spec = pl.BlockSpec((FWD_CHUNK, width), lambda i: (i, 0))
     return pl.pallas_call(
-        functools.partial(fwd_kernel, n_stages, n_chunks, TILE),
+        functools.partial(fwd_kernel, n_stages, n_chunks, FWD_TILE),
         grid=(n_chunks,),
         out_shape=jax.ShapeDtypeStruct((rows, width), jnp.bfloat16),
         in_specs=[row_spec, pl.BlockSpec((width, ff), lambda i: (0, 0)), pl.BlockSpec((ff, width), lambda i: (0, 0))],
         out_specs=row_spec,
         scratch_shapes=[
-            pltpu.VMEM((n_chunks, CHUNK, width), jnp.bfloat16),
-            pltpu.VMEM((n_chunks, CHUNK, width), jnp.bfloat16),
+            pltpu.VMEM((n_chunks, FWD_CHUNK, width), jnp.bfloat16),
+            pltpu.VMEM((n_chunks, FWD_CHUNK, width), jnp.bfloat16),
             pltpu.SemaphoreType.DMA((n_chunks,)),
             pltpu.SemaphoreType.DMA((n_chunks,)),
         ],
@@ -587,27 +589,35 @@
     )(flipped, dpre_own, hid_own, grad_own, grad_up, grad_down)
 
 
-def adam_kernel(n_reps, scale_ref, master_ref, first_ref, second_ref, sum_ref, new_master, new_first, new_second, new_bf):
-    result, first_mom, second_mom = adamw_update(master_ref[...], first_ref[...], second_ref[...], sum_ref[...] / n_reps, scale_ref[0], scale_ref[1])
-    new_master[...] = result
-    new_first[...] = first_mom
-    new_second[...] = second_mom
-    new_bf[...] = result.astype(jnp.bfloat16)
-
-
-def adam(n_reps, scales, master, first_mom, second_mom, grad_sum):
-    rows, cols = master.shape
-    block = pl.BlockSpec((rows // ADAM_BLOCKS, cols), lambda i: (i, 0))
-    full = jax.ShapeDtypeStruct(master.shape, jnp.float32)
+def adam_kernel(n_reps, scale_ref, *refs):
+    for start in range(2):
+        master_ref, first_ref, second_ref, sum_ref = refs[4 * start : 4 * start + 4]
+        new_master, new_first, new_second, new_bf = refs[8 + 4 * start : 12 + 4 * start]
+        result, first_mom, second_mom = adamw_update(master_ref[...], first_ref[...], second_ref[...], sum_ref[...] / n_reps, scale_ref[0], scale_ref[1])
+        new_master[...] = result
+        new_first[...] = first_mom
+        new_second[...] = second_mom
+        new_bf[...] = result.astype(jnp.bfloat16)
+
+
+def adam(n_reps, scales, up_arrays, down_arrays):
+    in_specs, out_specs, shapes = [], [], []
+    for arrays in (up_arrays, down_arrays):
+        rows, cols = arrays[0].shape
+        block = pl.BlockSpec((rows // ADAM_BLOCKS, cols), lambda i: (i, 0))
+        full = jax.ShapeDtypeStruct((rows, cols), jnp.float32)
+        in_specs += [block] * 4
+        out_specs += [block] * 4
+        shapes += [full, full, full, jax.ShapeDtypeStruct((rows, cols), jnp.bfloat16)]
     return pl.pallas_call(
         functools.partial(adam_kernel, n_reps),
         grid=(ADAM_BLOCKS,),
-        out_shape=(full, full, full, jax.ShapeDtypeStruct(master.shape, jnp.bfloat16)),
-        in_specs=[pl.BlockSpec(memory_space=pltpu.SMEM), block, block, block, block],
-        out_specs=(block, block, block, block),
-        compiler_params=pltpu.CompilerParams(dimension_semantics=('arbitrary',), vmem_limit_bytes=60 * 2**20),
+        out_shape=tuple(shapes),
+        in_specs=[pl.BlockSpec(memory_space=pltpu.SMEM), *in_specs],
+        out_specs=tuple(out_specs),
+        compiler_params=pltpu.CompilerParams(dimension_semantics=('arbitrary',), vmem_limit_bytes=67043328),
         name='adam',
-    )(scales, master, first_mom, second_mom, grad_sum)
+    )(scales, *up_arrays, *down_arrays)
 
 
 def solution(mesh):
@@ -621,8 +631,9 @@
         grad_norm = jnp.sqrt(lax.psum(jnp.sum(squares), 'stage'))
         clip_scale = jnp.minimum(1.0, max_norm / (grad_norm + NORM_EPS))
         scales = jnp.stack([clip_scale, learn_rate])
-        new_up, new_m1_up, new_m2_up, up_bf = adam(n_reps, scales, master_up[0], mom1_up[0], mom2_up[0], sum_up)
-        new_down, new_m1_down, new_m2_down, down_bf = adam(n_reps, scales, master_down[0], mom1_down[0], mom2_down[0], sum_down)
+        new_up, new_m1_up, new_m2_up, up_bf, new_down, new_m1_down, new_m2_down, down_bf = adam(
+            n_reps, scales, (master_up[0], mom1_up[0], mom2_up[0], sum_up), (master_down[0], mom1_down[0], mom2_down[0], sum_down)
+        )
         stage_out = forward(n_stages, next_batch[0], up_bf, down_bf)
         return (new_up[None], new_down[None], new_m1_up[None], new_m1_down[None], new_m2_up[None], new_m2_down[None], stage_out[None, None])
 

time: 532 us -> 525 us (0.987)
  Pallas kernels: 487 us -> 480 us
    pallas_call x1, Pallas kernels: 56.6 us -> 51.3 us  [forward(): pl.pallas_call(functools.partial(fwd_kernel, n_stages, n_chunks, FWD_TILE...]
    pallas_call x2 -> x1, Pallas kernels: 48.4 us -> 46.5 us  [adam(): pl.pallas_call(functools.partial(adam_kernel, n_reps), grid=(ADAM_BLOCKS,...]
where the time goes in v3:
time: 525 us; the launch traced here: 524 us
  Pallas kernels  480 us (91%)
  blocking collectives  36 us (7%)
    pallas_call x1, Pallas kernels, sum_grads(): pl.pallas_call(functools.partial(sum_kernel, n_chunks, SUM_SKEW, n_reps),...  328 us
    pallas_call x1, Pallas kernels, backward(): pl.pallas_call(functools.partial(back_kernel, n_stages, n_chunks, TILE),...  54.1 us
    pallas_call x1, Pallas kernels, forward(): pl.pallas_call(functools.partial(fwd_kernel, n_stages, n_chunks, FWD_TILE...  51.3 us
    pallas_call x1, Pallas kernels, adam(): pl.pallas_call(functools.partial(adam_kernel, n_reps), grid=(ADAM_BLOCKS,...  46.5 us
    psum x1, blocking collectives, local_step(): grad_norm = jnp.sqrt(lax.psum(jnp.sum(squares), 'stage'))  36 us

profile of v3, /device:TPU:3, one launch (start us, length us, event | category | flops | bytes accessed | tf_op | source)
XLA Modules:
  0.0 524.3 jit_solution(115124291022865676)
XLA Ops:
  1.9 54.1 %backward.1 = (bf16[24,2048,128]{2,1,0:T(8,128)(2,1)}, bf16[24,2048,128]{2,1,0:T(8,128)(2,1)}, bf16[2048,768]{1,0:T(8,128)(2,1)}, bf16[768,2048]{1,0:T(8,128)(2,1)}) custom-call(bf16[2048,768]{1,0:T(8,128)(2,1)} %bitcast.31, f32[768,3072]{1,0:T(8,128)} %bitcast.20, f32[3072,768]{1,0:T(8,128)} %bitcast.22, bf16[2048,768]{1,0:T(8,128)(2,1)} %loss_ref.1), custom_call_target="tpu_custom_call" | custom-call | tf_op jit(solution)/shard_map/backward/pallas_call | solution.py:180
  56.0 328.1 %sum_grads.1 = (f32[768,3072]{1,0:T(8,128)}, f32[3072,768]{1,0:T(8,128)}, f32[8,128]{1,0:T(8,128)}) custom-call(bf16[768,2048]{1,0:T(8,128)(2,1)} %get-tuple-element.22.flip_ref, bf16[24,2048,128]{2,1,0:T(8,128)(2,1)} %get-tuple-element.23.dpre_hbm, bf16[24,2048,128]{2,1,0:T(8,128)(2,1)} %get-tuple-element.24.hid_hbm, ...), custom_call_target="tpu_custom_call" | custom-call | tf_op jit(solution)/shard_map/sum_grads/pallas_call | solution.py:560
  384.2 1.3 reduce_sum.9
  385.4 36.0 %psum.7 = f32[]{:T(128)} all-reduce(f32[]{:T(128)} %reduce_sum.9), channel_id=1, replica_groups=mesh['data'=8,'stage'=4] {'stage'}, use_global_device_ids=true, to_apply=%region_1.0 | all-reduce | flops 1 | bytes 8 | tf_op jit(solution)/shard_map/psum | solution.py:631
  422.2 0.6 pad_maximum_fusion.scale_ref
  422.8 46.5 %adam.1 = (f32[768,3072]{1,0:T(8,128)}, f32[768,3072]{1,0:T(8,128)}, f32[768,3072]{1,0:T(8,128)}, bf16[768,3072]{1,0:T(8,128)(2,1)}, f32[3072,768]{1,0:T(8,128)}...) custom-call(f32[2]{0:T(128)} %pad_maximum_fusion.scale_ref, f32[768,3072]{1,0:T(8,128)} %bitcast.21, ...), custom_call_target="tpu_custom_call" | custom-call | tf_op jit(solution)/shard_map/adam/pallas_call | solution.py:612
  469.3 51.3 %forward.1 = bf16[2048,768]{1,0:T(8,128)(2,1)} custom-call(bf16[2048,768]{1,0:T(8,128)(2,1)} %bitcast.32, bf16[768,3072]{1,0:T(8,128)(2,1)} %get-tuple-element.35.up_ref, bf16[3072,768]{1,0:T(8,128)(2,1)} %get-tuple-element.36.down_ref), custom_call_target="tpu_custom_call" | custom-call | tf_op jit(solution)/shard_map/forward/pallas_call | solution.py:265
  520.6 3.8 copy.23
